TPU v7x, 32 devices: a whole 2x2x4 slice. The times are simulated.
32 devices in a mesh: row: 4 (over y, core), col: 8 (over z, x).
Axes of the slice: x: 2, y: 2, z: 4, core: 2. Of those that a mesh axis runs over, the one named last changes fastest.
Arguments:
- obs_cell: int32 [32, 16, 32, 128], P(('row', 'col')), may hold values from 0 to 8388607, as said below
- obs_value: bfloat16 [32, 16, 32, 128], P(('row', 'col')), may hold values from -6 to 6
- obs_weight: bfloat16 [32, 16, 32, 128], P(('row', 'col')), may hold values from 0.5 to 2
- obs_count: int32 [32, 16, 32], P(('row', 'col')), may hold values from 0 to 128, as said below
- kappa_field: float32 [2048, 4096], P('row', 'col'), may hold values from 0.2 to 6
Outputs:
- solution_field: float32 [2048, 4096], P('row', 'col')
- residual: float32 [2048, 4096], P('row', 'col')
Inputs may be any that keep to these rules, and one draw needn't show every extreme that they name: `obs_cell`: block (s, t, d) holds observations for tile t of device d, where device d is number d // 8 along row and d % (8) along col, and tile t is number t // 4 among the device's tiles along rows and t % (4) along columns, each tile 128 by 128 cells; every slot of the block, padding included, names a cell of that tile as row * 4096 + column. Slots at positions obs_count and beyond are padding. For one owner device, chosen afresh in each draw, every block from every source and tile is full.
All inputs are finite; a program needn't handle non-finite values.
Results may differ from a plain program's by a relative error of at most 0.0029.
Values may be sent and summed in bfloat16 or wider, within the bound.
A program may use at most 64 MiB of HBM per device.

v0:
```python
import functools

import jax
import jax.numpy as jnp
from jax import lax
from jax.experimental import pallas as pl
from jax.experimental.pallas import tpu as pltpu
from jax.sharding import PartitionSpec as P

TILE = 128
ITERS = 3
HALO = 8
PAD = 2 * HALO
STRIP = 176
SOURCES = 32
GROUP = 8

smooth_weight = 0.05

MESH = pl.DeviceIdType.MESH


def greet_all(me, count, cols):
    barrier = pltpu.get_barrier_semaphore()

    def signal(k, carry):
        peer = lax.rem(me + k, count)
        pl.semaphore_signal(
            barrier, inc=1, device_id=(peer // cols, lax.rem(peer, cols)), device_id_type=MESH
        )
        return carry

    lax.fori_loop(1, count, signal, 0)


def await_all(count):
    pl.semaphore_wait(pltpu.get_barrier_semaphore(), count - 1)


def observe_kernel(
    rows, cols, code_ref, pair_ref, weight_ref, response_ref,
    code_in, pair_in, place_row, place_col, amounts, send_sems, recv_sems, own_sems,
):
    count, groups, each, slots = code_ref.shape
    me = lax.axis_index("row") * cols + lax.axis_index("col")
    own_code = pltpu.make_async_copy(code_ref.at[me], code_in.at[me], own_sems.at[0])
    own_pair = pltpu.make_async_copy(pair_ref.at[me], pair_in.at[me], own_sems.at[1])
    greet_all(me, count, cols)
    own_code.start()
    own_pair.start()
    await_all(count)
    buffers = ((code_ref, code_in), (pair_ref, pair_in))

    def copies(group, k, peer, slot):
        return [
            pltpu.make_async_remote_copy(
                src_ref=src.at[peer, group],
                dst_ref=dst.at[slot, group],
                send_sem=send_sems.at[group, which, k],
                recv_sem=recv_sems.at[group, which, k],
                device_id=(peer // cols, lax.rem(peer, cols)),
                device_id_type=MESH,
            )
            for which, (src, dst) in enumerate(buffers)
        ]

    for group in range(groups):

        def begin(k, carry, group=group):
            for copy in copies(group, k, lax.rem(me + k, count), me):
                copy.start()
            return carry

        lax.fori_loop(1, count, begin, 0)
    own_code.wait()
    own_pair.wait()

    bunch = min(SOURCES, count)
    chunk = bunch * slots
    offsets = (
        lax.broadcasted_iota(jnp.int32, (TILE, chunk), 0).astype(jnp.float32).astype(jnp.bfloat16)
    )
    one = jnp.ones((TILE, chunk), jnp.bfloat16)
    zero = jnp.zeros((TILE, chunk), jnp.bfloat16)
    across = weight_ref.shape[1] // TILE

    for group in range(groups):

        def finish(k, carry, group=group):
            source = lax.rem(me + count - k, count)
            for copy in copies(group, k, source, source):
                copy.wait()
            return carry

        lax.fori_loop(1, count, finish, 0)

        def decode(i, carry, group=group):
            some = pl.ds(i * 8, 8)
            code = code_in[some, group].astype(jnp.int32).reshape(8 * each, slots)
            here = pl.ds(pl.multiple_of(i * 8 * each, 8 * each), 8 * each)
            place_row[here, :] = (code >> 7).astype(jnp.float32)
            place_col[here, :] = (code & (TILE - 1)).astype(jnp.float32)
            pair = pair_in[some, group].astype(jnp.float32).reshape(16 * each, slots)
            amounts[pl.ds(pl.multiple_of(i * 16 * each, 16 * each), 16 * each), :] = pair
            return carry

        lax.fori_loop(0, count // 8, decode, 0, unroll=2)

        def bin_tile(at, carry, group=group):
            def part(i, total):
                def spread(ref, first, step):
                    piece = ref[pl.ds(i * (bunch * step) + first, bunch, stride=step), :]
                    line = jnp.concatenate([piece[n : n + 1] for n in range(bunch)], axis=1)
                    return jnp.broadcast_to(line.astype(jnp.bfloat16), (TILE, chunk))

                col_hot = jnp.where(spread(place_col, at, each) == offsets, one, zero)
                row_hit = spread(place_row, at, each) == offsets
                weight = spread(amounts, at, 2 * each)
                product = spread(amounts, at + each, 2 * each)
                stacked = jnp.concatenate(
                    [jnp.where(row_hit, weight, zero), jnp.where(row_hit, product, zero)], axis=0
                )
                return total + lax.dot_general(
                    stacked, col_hot, (((1,), (1,)), ((), ())), preferred_element_type=jnp.float32
                )

            total = lax.fori_loop(
                0, count // bunch, part, jnp.zeros((2 * TILE, TILE), jnp.float32)
            )
            tile = group * each + at
            where = (
                pl.ds(pl.multiple_of((tile // across) * TILE, TILE), TILE),
                pl.ds(pl.multiple_of((tile % across) * TILE, TILE), TILE),
            )
            weight_ref[where] = total[:TILE]
            response_ref[where] = total[TILE:]
            return carry

        lax.fori_loop(0, each, bin_tile, 0, unroll=4)


def smooth_kernel(
    rows, cols, b_ref, w_ref, k_ref, x_ref, r_ref,
    res, wgt, kap, live, inner, image, along, second, further, course,
    send_low, send_high, recv_low, recv_high, mine, sums,
    row_send, row_recv, col_send, col_recv, sum_send, sum_recv,
):
    count = rows * cols
    my_row, my_col = lax.axis_index("row"), lax.axis_index("col")
    me = my_row * cols + my_col
    height, width = b_ref.shape
    full = width + 128
    own = pl.ds(PAD, height)
    fields = ((b_ref, res), (w_ref, wgt), (k_ref, kap))
    tall = res.shape[0]

    for _, field in fields:
        field[0:PAD, :] = jnp.zeros((PAD, full), jnp.float32)
        field[PAD + height :, :] = jnp.zeros((tall - PAD - height, full), jnp.float32)
    inner[0:HALO, :] = jnp.zeros((HALO, full), jnp.float32)
    inner[PAD + height + HALO : 2 * PAD + height, :] = jnp.zeros((HALO, full), jnp.float32)
    recv_low[...] = jnp.zeros_like(recv_low)
    recv_high[...] = jnp.zeros_like(recv_high)
    greet_all(me, count, cols)

    def fill(i, carry):
        at = pl.multiple_of(i * 32, 32)
        for src, dst in fields:
            dst[pl.ds(PAD + at, 32), 0:width] = src[pl.ds(at, 32), :]
        return carry

    lax.fori_loop(0, height // 32, fill, 0)

    await_all(count)

    up, down = my_row > 0, my_row < rows - 1
    left, right = my_col > 0, my_col < cols - 1

    def row_copies(way):
        made = []
        for at, (src, dst) in enumerate(fields):
            if way == 0:
                source, target = src.at[pl.ds(0, HALO), :], dst.at[pl.ds(PAD + height, HALO), pl.ds(0, width)]
                where = (my_row - 1, my_col)
            else:
                source, target = src.at[pl.ds(height - HALO, HALO), :], dst.at[pl.ds(HALO, HALO), pl.ds(0, width)]
                where = (my_row + 1, my_col)
            made.append(
                pltpu.make_async_remote_copy(
                    src_ref=source, dst_ref=target,
                    send_sem=row_send.at[way, at], recv_sem=row_recv.at[way, at],
                    device_id=where, device_id_type=MESH,
                )
            )
        return made

    def col_copy(way):
        source, target, where = (
            (send_low, recv_high, (my_row, my_col - 1)),
            (send_high, recv_low, (my_row, my_col + 1)),
        )[way]
        return pltpu.make_async_remote_copy(
            src_ref=source, dst_ref=target, send_sem=col_send.at[way], recv_sem=col_recv.at[way],
            device_id=where, device_id_type=MESH,
        )

    for way, there in ((0, up), (1, down)):

        @pl.when(there)
        def _(way=way):
            for copy in row_copies(way):
                copy.start()

    for way, there in ((0, up), (1, down)):

        @pl.when(there)
        def _(way=way):
            for copy in row_copies(way):
                copy.wait_send()

        @pl.when((down, up)[way])
        def _(way=way):
            for copy in row_copies(way):
                copy.wait_recv()

    def pack(i, carry):
        at = pl.multiple_of(i * 128, 128)
        for which, (_, field) in enumerate(fields):
            low = field[pl.ds(at, 128), 0:128].T
            send_low[which * HALO : (which + 1) * HALO, pl.ds(at, 128)] = low[:HALO]
            high = field[pl.ds(at, 128), width - 128 : width].T
            send_high[which * HALO : (which + 1) * HALO, pl.ds(at, 128)] = high[128 - HALO :]
        return carry

    lax.fori_loop(0, tall // 128, pack, 0, unroll=True)
    for way, there in ((0, left), (1, right)):

        @pl.when(there)
        def _(way=way):
            col_copy(way).start()

    for way, there in ((0, left), (1, right)):

        @pl.when(there)
        def _(way=way):
            col_copy(way).wait_send()

        @pl.when((right, left)[way])
        def _(way=way):
            col_copy(way).wait_recv()

    gap = jnp.zeros((128 - 2 * HALO, 128), jnp.float32)

    def unpack(i, carry):
        at = pl.multiple_of(i * 128, 128)
        for which, (_, field) in enumerate(fields):
            part = slice(which * HALO, (which + 1) * HALO)
            both = jnp.concatenate(
                [recv_high[part, pl.ds(at, 128)], gap, recv_low[part, pl.ds(at, 128)]], axis=0
            )
            field[pl.ds(at, 128), width:full] = both.T
        return carry

    lax.fori_loop(0, tall // 128, unpack, 0, unroll=True)

    strips = (height + 2 * HALO) // STRIP
    top = jnp.where(up, HALO, PAD)
    bottom = PAD + height + jnp.where(down, HALO, 0)
    high_end = width + jnp.where(right, HALO, 0)
    low_begin = full - jnp.where(left, HALO, 0)

    def start_of(i):
        return pl.multiple_of(HALO + i * STRIP, 8)

    def prepare(i, carry):
        at = start_of(i)
        row = lax.broadcasted_iota(jnp.int32, (STRIP, full), 0) + at
        col = lax.broadcasted_iota(jnp.int32, (STRIP, full), 1)
        inside = (row >= top) & (row < bottom) & ((col < high_end) | (col >= low_begin))
        mask = jnp.where(inside, 1.0, 0.0).astype(jnp.float32)
        live[pl.ds(at, STRIP), :] = mask
        kap[pl.ds(at, STRIP), :] = jnp.where(inside, 4.0 + kap[pl.ds(at, STRIP), :], 0.0)
        return carry

    lax.fori_loop(0, strips, prepare, 0)

    def stencil(field, at):
        slab = field[pl.ds(pl.multiple_of(at - HALO, 8), STRIP + 2 * HALO), :]
        center = slab[HALO : HALO + STRIP]
        beside = slab[HALO + 1 : HALO + 1 + STRIP] + slab[HALO - 1 : HALO - 1 + STRIP]
        beside = beside + pltpu.roll(center, full - 1, axis=1) + pltpu.roll(center, 1, axis=1)
        here = pl.ds(at, STRIP)
        return kap[here, :] * center - live[here, :] * beside

    def operate(source, target):
        def first(i, carry):
            at = start_of(i)
            inner[pl.ds(at, STRIP), :] = stencil(source, at)
            return carry

        def last(i, carry):
            at = start_of(i)
            here = pl.ds(at, STRIP)
            target[here, :] = wgt[here, :] * source[here, :] + smooth_weight * stencil(inner, at)
            return carry

        lax.fori_loop(0, strips, first, 0)
        lax.fori_loop(0, strips, last, 0)

    lane = lax.broadcasted_iota(jnp.int32, (1, 128), 1)

    def copy_to(step, k, peer, slot):
        return pltpu.make_async_remote_copy(
            src_ref=mine.at[step], dst_ref=sums.at[step, slot],
            send_sem=sum_send.at[step, k], recv_sem=sum_recv.at[step, k],
            device_id=(peer // cols, lax.rem(peer, cols)), device_id_type=MESH,
        )

    def begin_products(step):
        def add(i, carry):
            norm, curve = carry
            here = pl.ds(pl.multiple_of(PAD + i * 32, 8), 32)
            a, c = res[here, 0:width], image[here, 0:width]
            aa, ac = a * a, a * c
            norm = norm + ((aa[:8] + aa[8:16]) + (aa[16:24] + aa[24:]))
            return norm, curve + ((ac[:8] + ac[8:16]) + (ac[16:24] + ac[24:]))

        zero = jnp.zeros((8, width), jnp.float32)
        norm, curve = lax.fori_loop(0, height // 32, add, (zero, zero))
        norm = jnp.sum(jnp.sum(norm, axis=0, keepdims=True), axis=1, keepdims=True)
        curve = jnp.sum(jnp.sum(curve, axis=0, keepdims=True), axis=1, keepdims=True)
        both = jnp.where(lane == 0, norm, jnp.where(lane == 1, curve, 0.0))
        mine[step] = both
        sums[step, me] = both

        def begin(k, carry):
            copy_to(step, k, lax.rem(me + k, count), me).start()
            return carry

        lax.fori_loop(1, count, begin, 0, unroll=True)

    def end_products(step):
        def finish(k, carry):
            source = lax.rem(me + count - k, count)
            copy_to(step, k, source, source).wait()
            return carry

        lax.fori_loop(1, count, finish, 0, unroll=True)
        total = jnp.sum(sums[step], axis=0)
        norm = jnp.sum(jnp.where(lane == 0, total, 0.0), axis=1, keepdims=True)
        curve = jnp.sum(jnp.where(lane == 1, total, 0.0), axis=1, keepdims=True)
        return norm, curve

    operate(res, image)
    begin_products(0)
    norm_now = alpha = None
    for step in range(ITERS):
        if step + 1 < ITERS:
            operate(image, second)
        norm_next, curvature = end_products(step)
        if step == 0:
            ratio = None
            alpha = norm_next / curvature
        else:
            ratio = norm_next / norm_now
            alpha = norm_next / (curvature - ratio * norm_next / alpha)
        norm_now = norm_next

        if step + 1 < ITERS:

            def recede(i, carry, step=step, ratio=ratio, alpha=alpha):
                here = pl.ds(pl.multiple_of(HALO + i * 48, 8), 48)
                way, path, next_path = res[here, :], image[here, :], second[here, :]
                old, old_image = way, path
                if step > 0:
                    way = way + ratio * course[here, :]
                    path = path + ratio * along[here, :]
                    next_path = next_path + ratio * further[here, :]
                course[here, :] = way
                along[here, :] = path
                further[here, :] = next_path
                res[here, :] = old - alpha * path
                image[here, :] = old_image - alpha * next_path
                return carry

            lax.fori_loop(0, (height + 2 * HALO) // 48, recede, 0)
            begin_products(step + 1)

        def advance(i, carry, step=step, ratio=ratio, alpha=alpha):
            at = pl.multiple_of(i * 32, 32)
            here = pl.ds(pl.multiple_of(PAD + at, 8), 32)
            rows_here = pl.ds(at, 32)
            if step + 1 < ITERS:
                moved = alpha * course[here, 0:width]
            else:
                moved = alpha * (res[here, 0:width] + ratio * course[here, 0:width])
                r_ref[rows_here, :] = res[here, 0:width] - alpha * (
                    image[here, 0:width] + ratio * along[here, 0:width]
                )
            x_ref[rows_here, :] = moved if step == 0 else x_ref[rows_here, :] + moved
            return carry

        lax.fori_loop(0, height // 32, advance, 0)


def per_device(rows, cols, obs_cell, obs_value, obs_weight, obs_count, kappa_field):
    count = rows * cols
    height, width = kappa_field.shape
    tiles, _, slots = obs_cell.shape[1:]
    cell = obs_cell[0]
    local = (cell // (width * cols) % TILE) * TILE + cell % TILE
    alive = jnp.arange(slots, dtype=jnp.int32) < obs_count[0][:, :, None]
    code = jnp.where(alive, local, -1).astype(jnp.int16).transpose(1, 0, 2)
    product = (obs_weight[0].astype(jnp.float32) * obs_value[0].astype(jnp.float32)).astype(jnp.bfloat16)
    groups = tiles // GROUP
    code = code.reshape(count, groups, GROUP, slots)
    pair = jnp.concatenate(
        [
            array.transpose(1, 0, 2).reshape(count, groups, GROUP, slots)
            for array in (obs_weight[0], product)
        ],
        axis=2,
    )

    in_vmem = pl.BlockSpec(memory_space=pltpu.VMEM)
    field = jax.ShapeDtypeStruct((height, width), jnp.float32)
    weight_field, response = pl.pallas_call(
        functools.partial(observe_kernel, rows, cols),
        out_shape=(field, field),
        in_specs=[in_vmem] * 2,
        out_specs=(in_vmem,) * 2,
        scratch_shapes=[
            pltpu.VMEM(code.shape, code.dtype),
            pltpu.VMEM(pair.shape, pair.dtype),
            pltpu.VMEM((count * GROUP, slots), jnp.float32),
            pltpu.VMEM((count * GROUP, slots), jnp.float32),
            pltpu.VMEM((count * GROUP * 2, slots), jnp.float32),
            pltpu.SemaphoreType.DMA((groups, 2, count)),
            pltpu.SemaphoreType.DMA((groups, 2, count)),
            pltpu.SemaphoreType.DMA((2,)),
        ],
        compiler_params=pltpu.CompilerParams(
            collective_id=0, has_side_effects=True, vmem_limit_bytes=32 << 20
        ),
        name="observe",
    )(code, pair)

    full = width + 128
    tall = -(-(height + 2 * PAD) // 128) * 128
    extended = pltpu.VMEM((tall, full), jnp.float32)
    edge = pltpu.VMEM((3 * HALO, tall), jnp.float32)
    return pl.pallas_call(
        functools.partial(smooth_kernel, rows, cols),
        out_shape=(field, field),
        in_specs=[in_vmem] * 3,
        out_specs=(in_vmem,) * 2,
        scratch_shapes=[extended] * 10
        + [edge] * 4
        + [
            pltpu.VMEM((ITERS, 1, 128), jnp.float32),
            pltpu.VMEM((ITERS, count, 1, 128), jnp.float32),
            pltpu.SemaphoreType.DMA((2, 3)),
            pltpu.SemaphoreType.DMA((2, 3)),
            pltpu.SemaphoreType.DMA((2,)),
            pltpu.SemaphoreType.DMA((2,)),
            pltpu.SemaphoreType.DMA((ITERS, count)),
            pltpu.SemaphoreType.DMA((ITERS, count)),
        ],
        compiler_params=pltpu.CompilerParams(collective_id=1, has_side_effects=True, vmem_limit_bytes=32 << 20),
        name="smoothing",
    )(response, weight_field, kappa_field)


def solution(mesh):
    placed = (
        P(("row", "col"), None, None, None),
        P(("row", "col"), None, None, None),
        P(("row", "col"), None, None, None),
        P(("row", "col"), None, None),
        P("row", "col"),
    )
    return jax.shard_map(
        functools.partial(per_device, mesh.shape["row"], mesh.shape["col"]),
        mesh=mesh,
        in_specs=placed,
        out_specs=(P("row", "col"), P("row", "col")),
        check_vma=False,
    )
```

profile of v0, /device:TPU:0, one launch (start us, length us, event | category | flops | bytes accessed | tf_op | source)
XLA Modules:
  0.0 63.0 jit_solution(686348896078004275)
XLA Ops:
  0.6 0.0 copy-start.1
  0.6 0.0 copy-start.2
  0.7 1.4 %fusion.10 = s16[32,16,128]{2,0,1:T(8,128)(2,1)S(1)} fusion(s32[1,16,32,128]{3,2,1,0:T(8,128)} %param.5, s32[16,32]{1,0:T(8,128)} %bitcast.47), kind=kLoop, calls=%fused_computation.27 | loop fusion | flops 2555904 | bytes 395264 | tf_op jit(solution)/shard_map/transpose | solution.py:413
  2.0 0.0 copy-start
  2.0 0.1 copy.13
  2.1 0.0 copy-done.1
  2.1 0.0 copy-done.2
  2.1 0.1 copy_bitcast_fusion
  2.3 26.9 %observe.1 = (f32[512,512]{1,0:T(8,128)S(1)}, f32[512,512]{1,0:T(8,128)S(1)}) custom-call(s16[32,2,8,128]{3,2,1,0:T(8,128)(2,1)S(1)} %bitcast.45, bf16[32,2,16,128]{3,2,1,0:T(8,128)(2,1)S(1)} %pad_maximum_fusion.pair_ref), custom_call_target="tpu_custom_call" | custom-call | tf_op jit(solution)/shard_map/observe/pallas_call | solution.py:427
  29.2 0.0 copy-done
  29.2 31.8 %smoothing.1 = (f32[512,512]{1,0:T(8,128)S(1)}, f32[512,512]{1,0:T(8,128)S(1)}) custom-call(f32[512,512]{1,0:T(8,128)S(1)} %get-tuple-element.4.b_ref, f32[512,512]{1,0:T(8,128)S(1)} %get-tuple-element.5.w_ref, f32[512,512]{1,0:T(8,128)S(1)} %copy-done), custom_call_target="tpu_custom_call" | custom-call | tf_op jit(solution)/shard_map/smoothing/pallas_call | solution.py:452
  61.0 1.0 %copy.16 = f32[512,512]{1,0:T(8,128)} copy(f32[512,512]{1,0:T(8,128)S(1)} %get-tuple-element.10) | data formatting | bytes 2097152
  62.0 1.0 %copy.17 = f32[512,512]{1,0:T(8,128)} copy(f32[512,512]{1,0:T(8,128)S(1)} %get-tuple-element.11) | data formatting | bytes 2097152
  (2 shorter events, 0.1 us)
Async XLA Ops:
  0.6 1.4 %copy-start.1 = (bf16[1,16,32,128]{3,2,1,0:T(8,128)(2,1)S(1)}, bf16[1,16,32,128]{3,2,1,0:T(8,128)(2,1)}, u32[]{:S(2)}) copy-start(bf16[1,16,32,128]{3,2,1,0:T(8,128)(2,1)} %param.7) | copy-start | bytes 393220
  0.6 1.4 %copy-start.2 = (bf16[1,16,32,128]{3,2,1,0:T(8,128)(2,1)S(1)}, bf16[1,16,32,128]{3,2,1,0:T(8,128)(2,1)}, u32[]{:S(2)}) copy-start(bf16[1,16,32,128]{3,2,1,0:T(8,128)(2,1)} %param.6) | copy-start | bytes 393220
  2.0 27.2 %copy-start = (f32[512,512]{1,0:T(8,128)S(1)}, f32[512,512]{1,0:T(8,128)}, u32[]{:S(2)}) copy-start(f32[512,512]{1,0:T(8,128)} %k_ref.1) | copy-start | bytes 3145732
where the time goes:
time: 63.1 us; the launch traced here: 63 us
  Pallas kernels  58.7 us (93%)
  local copies, waits for them, and re-layouts  2.12 us (3%)
  other arithmetic  1.44 us (2%)
  between operations  0.72 us (1%)
    pallas_call x1, Pallas kernels, per_device(): pl.pallas_call(functools.partial(smooth_kernel, rows, cols), out_shape=(f...  31.8 us
    pallas_call x1, Pallas kernels, per_device(): pl.pallas_call(functools.partial(observe_kernel, rows, cols), out_shape=(...  26.9 us
    unnamed x8, local copies, waits for them, and re-layouts  1.96 us
    transpose x1, other arithmetic, per_device(): code = jnp.where(alive, local, -1).astype(jnp.int16).transpose(1, 0, 2)  1.35 us

commit v1 on v0

--- a/solution.py
+++ b/solution.py
@@ -12,8 +12,11 @@
 HALO = 8
 PAD = 2 * HALO
 STRIP = 176
-SOURCES = 32
 GROUP = 8
+LANES = 128
+MARGIN = 16
+BAND = 16
+LIMIT = 2000.0
 
 smooth_weight = 0.05
 
@@ -35,108 +38,6 @@
 
 def await_all(count):
     pl.semaphore_wait(pltpu.get_barrier_semaphore(), count - 1)
-
-
-def observe_kernel(
-    rows, cols, code_ref, pair_ref, weight_ref, response_ref,
-    code_in, pair_in, place_row, place_col, amounts, send_sems, recv_sems, own_sems,
-):
-    count, groups, each, slots = code_ref.shape
-    me = lax.axis_index("row") * cols + lax.axis_index("col")
-    own_code = pltpu.make_async_copy(code_ref.at[me], code_in.at[me], own_sems.at[0])
-    own_pair = pltpu.make_async_copy(pair_ref.at[me], pair_in.at[me], own_sems.at[1])
-    greet_all(me, count, cols)
-    own_code.start()
-    own_pair.start()
-    await_all(count)
-    buffers = ((code_ref, code_in), (pair_ref, pair_in))
-
-    def copies(group, k, peer, slot):
-        return [
-            pltpu.make_async_remote_copy(
-                src_ref=src.at[peer, group],
-                dst_ref=dst.at[slot, group],
-                send_sem=send_sems.at[group, which, k],
-                recv_sem=recv_sems.at[group, which, k],
-                device_id=(peer // cols, lax.rem(peer, cols)),
-                device_id_type=MESH,
-            )
-            for which, (src, dst) in enumerate(buffers)
-        ]
-
-    for group in range(groups):
-
-        def begin(k, carry, group=group):
-            for copy in copies(group, k, lax.rem(me + k, count), me):
-                copy.start()
-            return carry
-
-        lax.fori_loop(1, count, begin, 0)
-    own_code.wait()
-    own_pair.wait()
-
-    bunch = min(SOURCES, count)
-    chunk = bunch * slots
-    offsets = (
-        lax.broadcasted_iota(jnp.int32, (TILE, chunk), 0).astype(jnp.float32).astype(jnp.bfloat16)
-    )
-    one = jnp.ones((TILE, chunk), jnp.bfloat16)
-    zero = jnp.zeros((TILE, chunk), jnp.bfloat16)
-    across = weight_ref.shape[1] // TILE
-
-    for group in range(groups):
-
-        def finish(k, carry, group=group):
-            source = lax.rem(me + count - k, count)
-            for copy in copies(group, k, source, source):
-                copy.wait()
-            return carry
-
-        lax.fori_loop(1, count, finish, 0)
-
-        def decode(i, carry, group=group):
-            some = pl.ds(i * 8, 8)
-            code = code_in[some, group].astype(jnp.int32).reshape(8 * each, slots)
-            here = pl.ds(pl.multiple_of(i * 8 * each, 8 * each), 8 * each)
-            place_row[here, :] = (code >> 7).astype(jnp.float32)
-            place_col[here, :] = (code & (TILE - 1)).astype(jnp.float32)
-            pair = pair_in[some, group].astype(jnp.float32).reshape(16 * each, slots)
-            amounts[pl.ds(pl.multiple_of(i * 16 * each, 16 * each), 16 * each), :] = pair
-            return carry
-
-        lax.fori_loop(0, count // 8, decode, 0, unroll=2)
-
-        def bin_tile(at, carry, group=group):
-            def part(i, total):
-                def spread(ref, first, step):
-                    piece = ref[pl.ds(i * (bunch * step) + first, bunch, stride=step), :]
-                    line = jnp.concatenate([piece[n : n + 1] for n in range(bunch)], axis=1)
-                    return jnp.broadcast_to(line.astype(jnp.bfloat16), (TILE, chunk))
-
-                col_hot = jnp.where(spread(place_col, at, each) == offsets, one, zero)
-                row_hit = spread(place_row, at, each) == offsets
-                weight = spread(amounts, at, 2 * each)
-                product = spread(amounts, at + each, 2 * each)
-                stacked = jnp.concatenate(
-                    [jnp.where(row_hit, weight, zero), jnp.where(row_hit, product, zero)], axis=0
-                )
-                return total + lax.dot_general(
-                    stacked, col_hot, (((1,), (1,)), ((), ())), preferred_element_type=jnp.float32
-                )
-
-            total = lax.fori_loop(
-                0, count // bunch, part, jnp.zeros((2 * TILE, TILE), jnp.float32)
-            )
-            tile = group * each + at
-            where = (
-                pl.ds(pl.multiple_of((tile // across) * TILE, TILE), TILE),
-                pl.ds(pl.multiple_of((tile % across) * TILE, TILE), TILE),
-            )
-            weight_ref[where] = total[:TILE]
-            response_ref[where] = total[TILE:]
-            return carry
-
-        lax.fori_loop(0, each, bin_tile, 0, unroll=4)
 
 
 def smooth_kernel(
@@ -403,48 +304,605 @@
         lax.fori_loop(0, height // 32, advance, 0)
 
 
+def edge_and_inner(down, across):
+    edge = 2 * across + 2 * (down - 2)
+    return edge, (down - 2) * (across - 2)
+
+
+def edge_tile(e, down, across):
+    side = e - across
+    last = across + 2 * (down - 2)
+    row = jnp.where(e < across, 0, jnp.where(e < last, 1 + side // 2, down - 1))
+    col = jnp.where(e < across, e, jnp.where(e < last, lax.rem(side, 2) * (across - 1), e - last))
+    return row, col
+
+
+def inner_tile(e, down, across):
+    return 1 + e // (across - 2), 1 + lax.rem(e, across - 2)
+
+
+def split(value, size):
+    if size & (size - 1) == 0:
+        return lax.shift_right_logical(value, size.bit_length() - 1), value & (size - 1)
+    return lax.div(value, size), lax.rem(value, size)
+
+
+def flip(place, code, size):
+    total, unit = 0, 1
+    while unit < size:
+        total = total + unit * lax.rem(place // unit + code // unit, 2)
+        unit *= 2
+    return total
+
+
+def field_kernel(
+    rows, cols, cell_hbm, value_hbm, weight_hbm, count_ref, kappa_hbm,
+    bw, first, second, third, coef, good,
+    cell_in, value_in, weight_in, cell_wide, value_wide, weight_wide,
+    code_out, pair_out, code_out_inner, pair_out_inner,
+    code_in, pair_in, code_in_inner, pair_in_inner,
+    place_row, place_col, amounts, kap, mid,
+    low_out, high_out, low_in, high_in, kap_low_out, kap_high_out, kap_low_in, kap_high_in,
+    mine, sums,
+    load_sems, send_sem, recv_sems, halo_send, halo_recv, sum_send, sum_recv,
+):
+    count = rows * cols
+    my_row, my_col = lax.axis_index("row"), lax.axis_index("col")
+    me = my_row * cols + my_col
+    height, width = kappa_hbm.shape
+    down, across = height // TILE, width // TILE
+    tiles = down * across
+    slots = code_in.shape[2]
+    edges, inners = edge_and_inner(down, across)
+    pitch = cell_wide.shape[0] // tiles
+    bottom = MARGIN + height
+    lane = lax.broadcasted_iota(jnp.int32, (1, LANES), 1)
+
+    loads = [
+        pltpu.make_async_copy(cell_hbm, cell_in, load_sems.at[0]),
+        pltpu.make_async_copy(value_hbm, value_in, load_sems.at[1]),
+        pltpu.make_async_copy(weight_hbm, weight_in, load_sems.at[2]),
+    ]
+    kappa_loads = [
+        pltpu.make_async_copy(
+            kappa_hbm.at[:, pl.ds(c * LANES, LANES)], kap.at[c, pl.ds(MARGIN, height), :], load_sems.at[3 + c]
+        )
+        for c in range(across)
+    ]
+    for load in loads + kappa_loads:
+        load.start()
+
+    for ref in (low_in, high_in, kap_low_in, kap_high_in):
+        ref[...] = jnp.zeros_like(ref)
+    strip = jnp.zeros((MARGIN, LANES), jnp.float32)
+    for c in range(across):
+        for field in (bw.at[0], bw.at[1], kap):
+            field[c, 0:MARGIN, :] = strip
+            field[c, bottom : bottom + MARGIN, :] = strip
+    greet_all(me, count, cols)
+
+    for field in (bw.at[0], bw.at[1], kap):
+        field[across, 0:MARGIN, :] = strip
+        field[across, bottom : bottom + MARGIN, :] = strip
+    for c in range(across + 1):
+        for field in (mid, first, second):
+            field[c, 0:8, :] = strip[:8]
+            field[c, bottom + 8 : bottom + 16, :] = strip[:8]
+
+    def person(k):
+        code_col, code_row = k // rows, lax.rem(k, rows)
+        return flip(my_row, code_row, rows), flip(my_col, code_col, cols)
+
+    for load in loads:
+        load.wait()
+
+    def widen(t, carry):
+        here = pl.ds(pl.multiple_of(t * count, 8), count)
+        there = pl.ds(pl.multiple_of(t * pitch, 8), count)
+        cell_wide[there, :] = cell_in[here, :]
+        weight = weight_in[here, :].astype(jnp.float32)
+        weight_wide[there, :] = weight
+        value_wide[there, :] = weight * value_in[here, :].astype(jnp.float32)
+        return carry
+
+    lax.fori_loop(0, tiles, widen, 0)
+    dest_lane = lax.broadcasted_iota(jnp.int32, count_ref.shape, 1)
+    slot_lane = lax.broadcasted_iota(jnp.int32, (tiles, slots), 1).astype(jnp.float32)
+    edge_ids = [t for t in range(tiles) if t // across in (0, down - 1) or t % across in (0, across - 1)]
+    inner_ids = [t for t in range(tiles) if t not in edge_ids]
+
+    def pick(value, ids):
+        parts, begin = [], 0
+        while begin < len(ids):
+            end = begin
+            while end + 1 < len(ids) and ids[end + 1] == ids[end] + 1:
+                end += 1
+            parts.append(value[ids[begin] : ids[end] + 1])
+            begin = end + 1
+        return jnp.concatenate(parts, axis=0) if len(parts) > 1 else parts[0]
+
+    def encode(k, carry):
+        row, col = person(k)
+        dest = row * cols + col
+        every = pl.ds(dest, tiles, stride=pitch)
+        cell = cell_wide[every, :]
+        upper, _ = split(cell, width * cols)
+        local = split(upper, TILE)[1] * TILE + split(cell, TILE)[1]
+        alive = jnp.sum(jnp.where(dest_lane == dest, count_ref[...], 0.0), axis=1, keepdims=True)
+        local = jnp.where(slot_lane < alive, local, -1)
+        weight, product = weight_wide[every, :], value_wide[every, :]
+        code_out[k] = pick(local, edge_ids).astype(jnp.int16)
+        pair_out[k] = jnp.concatenate([pick(weight, edge_ids), pick(product, edge_ids)], axis=0).astype(jnp.bfloat16)
+        code_out_inner[k] = pick(local, inner_ids).astype(jnp.int16)
+        pair_out_inner[k] = jnp.concatenate(
+            [pick(weight, inner_ids), pick(product, inner_ids)], axis=0
+        ).astype(jnp.bfloat16)
+        return carry
+
+    lax.fori_loop(0, count, encode, 0, unroll=2)
+    pieces = (
+        ((code_out, code_in), (pair_out, pair_in), edges, edge_tile),
+        ((code_out_inner, code_in_inner), (pair_out_inner, pair_in_inner), inners, inner_tile),
+    )
+    for piece in pieces:
+        for source, target in piece[:2]:
+            target[0] = source[0]
+    await_all(count)
+
+    bunch = GROUP
+    chunks = count // bunch
+
+    def send(piece, begin, end):
+        def one(k, carry):
+            place = person(k)
+            for which, (source, target) in enumerate(pieces[piece][:2]):
+                pltpu.make_async_remote_copy(
+                    src_ref=source.at[k], dst_ref=target.at[k],
+                    send_sem=send_sem.at[piece, which], recv_sem=recv_sems.at[k // bunch, piece, which],
+                    device_id=place, device_id_type=MESH,
+                ).start()
+            return carry
+
+        lax.fori_loop(begin, end, one, 0)
+
+    half = count // 2
+    send(0, half, count)
+    send(0, 1, half)
+    send(1, 1, half)
+    send(1, half, count)
+
+    def halo_copies(group, body, parts):
+        low_from, high_from, low_to, high_to = parts
+        up_rows, down_rows = pl.ds(MARGIN, 8), pl.ds(bottom - 8, 8)
+        above, below = pl.ds(MARGIN - 8, 8), pl.ds(bottom, 8)
+        main = pl.ds(LANES, height)
+        head, tail = pl.ds(0, LANES), pl.ds(LANES + height, LANES)
+        begin, end = pl.ds(0, LANES), pl.ds(height - LANES, LANES)
+        whole = pl.ds(0, height)
+        plan = [
+            (-1, 0, body(up_rows), body(below)),
+            (1, 0, body(down_rows), body(above)),
+            (0, -1, low_from.at[:, whole], high_to.at[:, main]),
+            (0, 1, high_from.at[:, whole], low_to.at[:, main]),
+            (-1, -1, low_from.at[:, begin], high_to.at[:, tail]),
+            (1, -1, low_from.at[:, end], high_to.at[:, head]),
+            (-1, 1, high_from.at[:, begin], low_to.at[:, tail]),
+            (1, 1, high_from.at[:, end], low_to.at[:, head]),
+        ]
+        made = []
+        for at, (dr, dc, source, target) in enumerate(plan):
+
+            def there(dr=dr, dc=dc):
+                ok = True
+                for step, place, size in ((dr, my_row, rows), (dc, my_col, cols)):
+                    if step < 0:
+                        ok = (place > 0) & ok
+                    if step > 0:
+                        ok = (place < size - 1) & ok
+                return ok
+
+            copy = pltpu.make_async_remote_copy(
+                src_ref=source, dst_ref=target,
+                send_sem=halo_send.at[group, at], recv_sem=halo_recv.at[group, at],
+                device_id=(my_row + dr, my_col + dc), device_id_type=MESH,
+            )
+            made.append((there(), there(-dr, -dc), copy))
+        return made
+
+    def start_halo(copies):
+        for goes, _, copy in copies:
+
+            @pl.when(goes)
+            def _(copy=copy):
+                copy.start()
+
+    def end_halo(copies):
+        for goes, comes, copy in copies:
+
+            @pl.when(goes)
+            def _(copy=copy):
+                copy.wait_send()
+
+            @pl.when(comes)
+            def _(copy=copy):
+                copy.wait_recv()
+
+    def pack(field, at, low, high):
+        for j in range(down):
+            here = pl.ds(MARGIN + j * TILE, TILE)
+            there = slice(j * TILE, (j + 1) * TILE)
+            low[at : at + 8, there] = field[0, here, :].T[:8]
+            high[at : at + 8, there] = field[across - 1, here, :].T[TILE - 8 :]
+
+    gap = jnp.zeros((LANES - 16, LANES), jnp.float32)
+
+    def unpack(field, at, low, high):
+        for j in range(-1, down + 1):
+            lanes = slice(LANES + j * TILE, LANES + (j + 1) * TILE)
+            both = jnp.concatenate([high[at : at + 8, lanes], gap, low[at : at + 8, lanes]], axis=0).T
+            if j < 0:
+                field[across, MARGIN - 8 : MARGIN, :] = both[TILE - 8 :]
+            elif j == down:
+                field[across, bottom : bottom + 8, :] = both[:8]
+            else:
+                field[across, MARGIN + j * TILE : MARGIN + (j + 1) * TILE, :] = both
+
+    kap_halo = halo_copies(
+        0, lambda part: kap.at[pl.ds(0, across), part, :], (kap_low_out, kap_high_out, kap_low_in, kap_high_in)
+    )
+    bw_halo = halo_copies(
+        1, lambda part: bw.at[:, pl.ds(0, across), part, :], (low_out, high_out, low_in, high_in)
+    )
+    for load in kappa_loads:
+        load.wait()
+    pack(kap, 0, kap_low_out, kap_high_out)
+    start_halo(kap_halo)
+
+    offsets = lax.broadcasted_iota(jnp.int32, (TILE, slots), 0).astype(jnp.float32).astype(jnp.bfloat16)
+    one = jnp.ones((TILE, slots), jnp.bfloat16)
+    zero = jnp.zeros((TILE, slots), jnp.bfloat16)
+
+    def bin_chunk(chunk, piece):
+        codes, pairs, some, locate = pieces[piece]
+        for which, (_, target) in enumerate((codes, pairs)):
+            begin = chunk * bunch + (1 if chunk == 0 else 0)
+            part = target.at[pl.ds(begin, (chunk + 1) * bunch - begin)]
+            pltpu.make_async_copy(part, part, recv_sems.at[chunk, piece, which]).wait()
+        for n in range(bunch):
+            code = codes[1][chunk * bunch + n].astype(jnp.int32)
+            place_row[n * some : (n + 1) * some, :] = (code >> 7).astype(jnp.float32)
+            place_col[n * some : (n + 1) * some, :] = (code & (TILE - 1)).astype(jnp.float32)
+            amounts[n * 2 * some : (n + 1) * 2 * some, :] = pairs[1][chunk * bunch + n].astype(jnp.float32)
+
+        def spread(ref, at):
+            return jnp.broadcast_to(ref[pl.ds(at, 1), :].astype(jnp.bfloat16), (TILE, slots))
+
+        def bin_tile(e, carry):
+            hot, weights, products = [], [], []
+            for n in range(bunch):
+                hot.append(jnp.where(spread(place_col, n * some + e) == offsets, one, zero))
+                hit = spread(place_row, n * some + e) == offsets
+                weights.append(jnp.where(hit, spread(amounts, n * 2 * some + e), zero))
+                products.append(jnp.where(hit, spread(amounts, n * 2 * some + some + e), zero))
+            stacked = jnp.concatenate(
+                [jnp.concatenate(products, axis=1), jnp.concatenate(weights, axis=1)], axis=0
+            )
+            total = lax.dot_general(
+                stacked, jnp.concatenate(hot, axis=1), (((1,), (1,)), ((), ())),
+                preferred_element_type=jnp.float32,
+            )
+            row, col = locate(e, down, across)
+            here = pl.ds(pl.multiple_of(MARGIN + row * TILE, 8), TILE)
+            if chunk == 0:
+                bw[0, col, here, :] = total[:TILE]
+                bw[1, col, here, :] = total[TILE:]
+            else:
+                bw[0, col, here, :] += total[:TILE]
+                bw[1, col, here, :] += total[TILE:]
+            return carry
+
+        lax.fori_loop(0, some, bin_tile, 0, unroll=4)
+
+    for chunk in range(chunks // 2):
+        bin_chunk(chunk, 0)
+        bin_chunk(chunk, 1)
+    for chunk in range(chunks // 2, chunks):
+        bin_chunk(chunk, 0)
+    for which in range(2):
+        pack(bw.at[which], 8 * which, low_out, high_out)
+    start_halo(bw_halo)
+    for chunk in range(chunks // 2, chunks):
+        bin_chunk(chunk, 1)
+    end_halo(kap_halo)
+    unpack(kap, 0, kap_low_in, kap_high_in)
+    for piece in range(2):
+        for which, (source, _) in enumerate(pieces[piece][:2]):
+            part = source.at[pl.ds(1, count - 1)]
+            pltpu.make_async_copy(part, part, send_sem.at[piece, which]).wait()
+    end_halo(bw_halo)
+    for which in range(2):
+        unpack(bw.at[which], 8 * which, low_in, high_in)
+
+    up, under = my_row > 0, my_row < rows - 1
+    live = ((lane < 8) & (my_col < cols - 1)) | ((lane >= LANES - 8) & (my_col > 0))
+
+    def inner(field, at, size, columns):
+        every = range(across + 1)
+        here = pl.ds(at, size)
+        center = [field[c, here, :] for c in every]
+        ahead = [pltpu.roll(x, 1, axis=1) for x in center]
+        behind = [pltpu.roll(x, LANES - 1, axis=1) for x in center]
+        result = []
+        for c in range(columns):
+            beside = field[c, pl.ds(at - 1, size), :] + field[c, pl.ds(at + 1, size), :]
+            beside = beside + jnp.where(lane == 0, ahead[c - 1], ahead[c])
+            beside = beside + jnp.where(lane == LANES - 1, behind[(c + 1) % (across + 1)], behind[c])
+            value = (4.0 + kap[c, here, :]) * center[c] - beside
+            result.append(jnp.where(live, value, 0.0) if c == across else value)
+        return result
+
+    response, weight = bw.at[0], bw.at[1]
+    outer = ((MARGIN - 8, up), (bottom, under))
+
+    def bands(body, carry):
+        def step(i, carry):
+            return body(pl.multiple_of(MARGIN + i * BAND, 8), carry)
+
+        return lax.fori_loop(0, height // BAND, step, carry)
+
+    def fold(value):
+        total = value[0:8]
+        for n in range(8, value.shape[0], 8):
+            total = total + value[n : n + 8]
+        return total
+
+    def apply_inner(source):
+        def body(at, carry):
+            square, energy = carry
+            for c, value in enumerate(inner(source, at, BAND, across + 1)):
+                here = pl.ds(at, BAND)
+                mid[c, here, :] = value
+                if c < across:
+                    x = source[c, here, :]
+                    xx = x * x
+                    square = square + fold(xx)
+                    energy = energy + fold(weight[c, here, :] * xx + smooth_weight * (value * value))
+            return square, energy
+
+        blank = jnp.zeros((8, LANES), jnp.float32)
+        result = bands(body, (blank, blank))
+        for at, there in outer:
+            for c, value in enumerate(inner(source, at, 8, across + 1)):
+                mid[c, pl.ds(at, 8), :] = jnp.where(there, value, 0.0)
+        return result
+
+    def apply_outer(source, target):
+        def store(at, size, there=None):
+            for c, value in enumerate(inner(mid, at, size, across + 1)):
+                here = pl.ds(at, size)
+                value = weight[c, here, :] * source[c, here, :] + smooth_weight * value
+                target[c, here, :] = value if there is None else jnp.where(there, value, 0.0)
+
+        def body(at, carry):
+            store(at, BAND)
+            return carry
+
+        bands(body, 0)
+        for at, there in outer:
+            store(at, 8, there)
+
+    moments = []
+    moments += apply_inner(response)
+    apply_outer(response, first)
+    moments += apply_inner(first)
+    apply_outer(first, second)
+    moments += apply_inner(second)
+
+    both = jnp.zeros((1, LANES), jnp.float32)
+    for at, value in enumerate(moments):
+        total = jnp.sum(jnp.sum(value, axis=0, keepdims=True), axis=1, keepdims=True)
+        both = jnp.where(lane == at, total, both)
+    mine[...] = both
+    sums[me] = both
+
+    def sum_copy(k, slot):
+        return pltpu.make_async_remote_copy(
+            src_ref=mine, dst_ref=sums.at[slot],
+            send_sem=sum_send.at[k], recv_sem=sum_recv.at[k],
+            device_id=person(k), device_id_type=MESH,
+        )
+
+    def begin(i, carry):
+        sum_copy(count - 1 - i, me).start()
+        return carry
+
+    lax.fori_loop(0, count - 1, begin, 0)
+
+    def last(at, carry):
+        for c, value in enumerate(inner(mid, at, BAND, across)):
+            here = pl.ds(at, BAND)
+            third[c, pl.ds(pl.multiple_of(at - MARGIN, 8), BAND), :] = (
+                weight[c, here, :] * second[c, here, :] + smooth_weight * value
+            )
+        return carry
+
+    bands(last, 0)
+
+    def finish(k, carry):
+        row, col = person(k)
+        sum_copy(k, row * cols + col).wait()
+        return carry
+
+    lax.fori_loop(1, count, finish, 0)
+    total = jnp.sum(sums[...], axis=0)
+    m = [jnp.sum(jnp.where(lane == at, total, 0.0), axis=1, keepdims=True) for at in range(6)]
+    scale = m[1] / m[0]
+    power, n = scale, [None, None]
+    for at in range(2, 6):
+        power = power * scale
+        n.append(m[at] / m[0] / power)
+    fall = n[2] - 1.0
+    bend = n[3] - n[2] * n[2]
+    alpha = fall / bend
+    a = 1.0 + alpha * n[2]
+    lead = n[2] - a * n[3] + alpha * n[4]
+    lead_size = n[2] + a * n[3] + alpha * n[4]
+    beta = alpha * lead / fall
+    d0, d1 = 1.0 + beta * n[2], a + beta
+    turn = d0 * n[3] - d1 * n[4] + alpha * n[5]
+    turn_size = d0 * n[3] + d1 * n[4] + alpha * n[5]
+    step = lead / turn
+    inverse = 1.0 / scale
+    powers = [inverse, inverse * inverse, inverse * inverse * inverse]
+    parts = [
+        (1.0 + alpha * n[2] + step * d0) * powers[0],
+        -(alpha + step * d1) * powers[1],
+        step * alpha * powers[2],
+        -(a + step * d0) * powers[0],
+        (alpha + step * d1) * powers[1],
+        -(step * alpha) * powers[2],
+    ]
+    for at, value in enumerate(parts):
+        coef[at : at + 1, :] = jnp.broadcast_to(value, (1, LANES))
+    coef[6:8, :] = jnp.zeros((2, LANES), jnp.float32)
+    sound = (fall * LIMIT >= n[2]) & (bend * LIMIT >= n[3])
+    sound = sound & (lead * LIMIT >= lead_size) & (turn * LIMIT >= turn_size)
+    sound = sound & (alpha * lead * (2.0 * LIMIT) >= 1.0 + a * a * n[2] + alpha * alpha * n[4])
+    good[...] = jnp.where(sound, 1, 0)
+
+
+def combine_kernel(bw, first, second, third, coef, x_hbm, r_hbm, x_out, r_out, sems):
+    across, height, _ = third.shape
+    band = height // 8
+    weights = [coef[at : at + 1, :] for at in range(6)]
+    copies = []
+    for i in range(8):
+        rows_here = pl.ds(i * band, band)
+
+        def body(j, carry, i=i):
+            at = pl.multiple_of(i * band + j * 32, 8)
+            for c in range(across):
+                here = pl.ds(MARGIN + at, 32)
+                values = [bw[0, c, here, :], first[c, here, :], second[c, here, :], third[c, pl.ds(at, 32), :]]
+                lanes = slice(c * LANES, (c + 1) * LANES)
+                x_out[pl.ds(at, 32), lanes] = (
+                    weights[0] * values[0] + weights[1] * values[1] + weights[2] * values[2]
+                )
+                r_out[pl.ds(at, 32), lanes] = (
+                    values[0] + weights[3] * values[1] + weights[4] * values[2] + weights[5] * values[3]
+                )
+            return carry
+
+        lax.fori_loop(0, band // 32, body, 0)
+        for at, (source, target) in enumerate(((x_out, x_hbm), (r_out, r_hbm))):
+            copy = pltpu.make_async_copy(source.at[rows_here], target.at[rows_here], sems.at[i, at])
+            copy.start()
+            copies.append(copy)
+    for copy in copies:
+        copy.wait()
+
+
 def per_device(rows, cols, obs_cell, obs_value, obs_weight, obs_count, kappa_field):
     count = rows * cols
     height, width = kappa_field.shape
     tiles, _, slots = obs_cell.shape[1:]
-    cell = obs_cell[0]
-    local = (cell // (width * cols) % TILE) * TILE + cell % TILE
-    alive = jnp.arange(slots, dtype=jnp.int32) < obs_count[0][:, :, None]
-    code = jnp.where(alive, local, -1).astype(jnp.int16).transpose(1, 0, 2)
-    product = (obs_weight[0].astype(jnp.float32) * obs_value[0].astype(jnp.float32)).astype(jnp.bfloat16)
-    groups = tiles // GROUP
-    code = code.reshape(count, groups, GROUP, slots)
-    pair = jnp.concatenate(
-        [
-            array.transpose(1, 0, 2).reshape(count, groups, GROUP, slots)
-            for array in (obs_weight[0], product)
+    down, across = height // TILE, width // TILE
+    edges, inners = edge_and_inner(down, across)
+    in_vmem = pl.BlockSpec(memory_space=pltpu.VMEM)
+    anywhere = pl.BlockSpec(memory_space=pl.ANY)
+    in_hbm = pl.BlockSpec(memory_space=pltpu.HBM)
+    tall = height + 2 * MARGIN
+    field = jax.ShapeDtypeStruct((height, width), jnp.float32)
+    wide = jax.ShapeDtypeStruct((across + 1, tall, LANES), jnp.float32)
+    pitch = count + 8
+    flat = (tiles * count, slots)
+    pitched = (tiles * pitch, slots)
+    edge = [
+        pltpu.VMEM((count, edges, slots), jnp.int16),
+        pltpu.VMEM((count, 2 * edges, slots), jnp.bfloat16),
+        pltpu.VMEM((count, inners, slots), jnp.int16),
+        pltpu.VMEM((count, 2 * inners, slots), jnp.bfloat16),
+    ]
+    bw, first, second, third, coef, good = pl.pallas_call(
+        functools.partial(field_kernel, rows, cols),
+        out_shape=(
+            jax.ShapeDtypeStruct((2, across + 1, tall, LANES), jnp.float32),
+            wide,
+            wide,
+            jax.ShapeDtypeStruct((across, height, LANES), jnp.float32),
+            jax.ShapeDtypeStruct((8, LANES), jnp.float32),
+            jax.ShapeDtypeStruct((1, 1), jnp.int32),
+        ),
+        in_specs=[anywhere] * 3 + [in_vmem, anywhere],
+        out_specs=(in_vmem,) * 6,
+        scratch_shapes=[
+            pltpu.VMEM(flat, jnp.int32),
+            pltpu.VMEM(flat, jnp.bfloat16),
+            pltpu.VMEM(flat, jnp.bfloat16),
+            pltpu.VMEM(pitched, jnp.int32),
+            pltpu.VMEM(pitched, jnp.float32),
+            pltpu.VMEM(pitched, jnp.float32),
+            *edge,
+            *edge,
+            pltpu.VMEM((GROUP * edges, slots), jnp.float32),
+            pltpu.VMEM((GROUP * edges, slots), jnp.float32),
+            pltpu.VMEM((GROUP * edges * 2, slots), jnp.float32),
+            pltpu.VMEM(wide.shape, jnp.float32),
+            pltpu.VMEM(wide.shape, jnp.float32),
+            pltpu.VMEM((16, height), jnp.float32),
+            pltpu.VMEM((16, height), jnp.float32),
+            pltpu.VMEM((16, height + 2 * LANES), jnp.float32),
+            pltpu.VMEM((16, height + 2 * LANES), jnp.float32),
+            pltpu.VMEM((8, height), jnp.float32),
+            pltpu.VMEM((8, height), jnp.float32),
+            pltpu.VMEM((8, height + 2 * LANES), jnp.float32),
+            pltpu.VMEM((8, height + 2 * LANES), jnp.float32),
+            pltpu.VMEM((1, LANES), jnp.float32),
+            pltpu.VMEM((count, 1, LANES), jnp.float32),
+            pltpu.SemaphoreType.DMA((3 + across,)),
+            pltpu.SemaphoreType.DMA((2, 2)),
+            pltpu.SemaphoreType.DMA((count // GROUP, 2, 2)),
+            pltpu.SemaphoreType.DMA((2, 8)),
+            pltpu.SemaphoreType.DMA((2, 8)),
+            pltpu.SemaphoreType.DMA((count,)),
+            pltpu.SemaphoreType.DMA((count,)),
         ],
-        axis=2,
+        compiler_params=pltpu.CompilerParams(
+            collective_id=0, has_side_effects=True, vmem_limit_bytes=30 << 20
+        ),
+        name="fields",
+    )(
+        obs_cell.reshape(flat), obs_value.reshape(flat), obs_weight.reshape(flat),
+        obs_count[0].astype(jnp.float32), kappa_field,
     )
 
+    def combine(bw, first, second, third, coef, kappa):
+        return pl.pallas_call(
+            combine_kernel,
+            out_shape=(field, field),
+            in_specs=[in_vmem] * 5,
+            out_specs=(in_hbm,) * 2,
+            scratch_shapes=[
+                pltpu.VMEM(field.shape, jnp.float32),
+                pltpu.VMEM(field.shape, jnp.float32),
+                pltpu.SemaphoreType.DMA((8, 2)),
+            ],
+            compiler_params=pltpu.CompilerParams(vmem_limit_bytes=16 << 20),
+            name="combine",
+        )(bw, first, second, third, coef)
+
+    def iterate(bw, first, second, third, coef, kappa):
+        own = bw[:, :across, MARGIN : MARGIN + height, :].transpose(0, 2, 1, 3).reshape(2, height, width)
+        return smooth(rows, cols, own[0], own[1], kappa)
+
+    return lax.cond(good[0, 0] > 0, combine, iterate, bw, first, second, third, coef, kappa_field)
+
+
+def smooth(rows, cols, response, weight_field, kappa_field):
+    count = rows * cols
+    height, width = kappa_field.shape
     in_vmem = pl.BlockSpec(memory_space=pltpu.VMEM)
     field = jax.ShapeDtypeStruct((height, width), jnp.float32)
-    weight_field, response = pl.pallas_call(
-        functools.partial(observe_kernel, rows, cols),
-        out_shape=(field, field),
-        in_specs=[in_vmem] * 2,
-        out_specs=(in_vmem,) * 2,
-        scratch_shapes=[
-            pltpu.VMEM(code.shape, code.dtype),
-            pltpu.VMEM(pair.shape, pair.dtype),
-            pltpu.VMEM((count * GROUP, slots), jnp.float32),
-            pltpu.VMEM((count * GROUP, slots), jnp.float32),
-            pltpu.VMEM((count * GROUP * 2, slots), jnp.float32),
-            pltpu.SemaphoreType.DMA((groups, 2, count)),
-            pltpu.SemaphoreType.DMA((groups, 2, count)),
-            pltpu.SemaphoreType.DMA((2,)),
-        ],
-        compiler_params=pltpu.CompilerParams(
-            collective_id=0, has_side_effects=True, vmem_limit_bytes=32 << 20
-        ),
-        name="observe",
-    )(code, pair)
-
     full = width + 128
     tall = -(-(height + 2 * PAD) // 128) * 128
     extended = pltpu.VMEM((tall, full), jnp.float32)

time: 63.1 us -> 64.7 us (1.025)
  local copies, waits for them, and re-layouts: 2.12 us -> 7.28 us
  Pallas kernels: 58.7 us -> 54.9 us
  other arithmetic: 1.44 us -> 0.7 us
    unnamed x8, local copies, waits for them, and re-layouts: 1.96 us -> 7.28 us
    pallas_call x2, Pallas kernels: 58.7 us -> 54.9 us  [the longest x1 51.3 us: per_device(): pl.pallas_call(functools.partial(field_kernel, rows, cols), out_shape=(ja...]
    transpose x2 -> x0, other arithmetic: 1.39 us -> none  [the longest x1 1.35 us: per_device(): code = jnp.where(alive, local, -1).astype(jnp.int16).transpose(1, 0, 2)]
    convert_element_type x0 -> x1, other arithmetic: none -> 0.7 us  [per_device(): obs_count[0].astype(jnp.float32)]
where the time goes in v1:
time: 64.7 us; the launch traced here: 64.3 us
  Pallas kernels  54.9 us (85%)
  local copies, waits for them, and re-layouts  7.28 us (11%)
  between operations  1.27 us (2%)
  other arithmetic  0.7 us (1%)
    pallas_call x1, Pallas kernels, per_device(): pl.pallas_call(functools.partial(field_kernel, rows, cols), out_shape=(ja...  51.3 us
    unnamed x8, local copies, waits for them, and re-layouts  7.28 us
    pallas_call x1, Pallas kernels, combine(): pl.pallas_call(combine_kernel, out_shape=(field, field), in_specs=[in_vme...  3.6 us

profile of v1, /device:TPU:0, one launch (start us, length us, event | category | flops | bytes accessed | tf_op | source)
XLA Modules:
  0.0 64.3 jit_solution(8063158652525418465)
XLA Ops:
  0.6 0.7 %convert_bitcast_fusion.count_ref = f32[16,32]{1,0:T(8,128)S(1)} fusion(s32[1,16,32]{2,1,0:T(8,128)} %param.10), kind=kLoop, calls=%fused_computation.3 | loop fusion | flops 512 | bytes 4096 | tf_op jit(solution)/shard_map/convert_element_type | solution.py:876
  1.3 0.0 copy-start
  1.3 0.9 %copy-done = s32[1,16,32,128]{3,2,1,0:T(8,128)S(1)} copy-done((s32[1,16,32,128]{3,2,1,0:T(8,128)S(1)}, s32[1,16,32,128]{3,2,1,0:T(8,128)}, u32[]{:S(2)}) %copy-start) | copy-done | bytes 262168
  2.3 0.0 copy-start.1
  2.3 0.9 %copy-done.1 = bf16[1,16,32,128]{3,2,1,0:T(8,128)(2,1)S(1)} copy-done((bf16[1,16,32,128]{3,2,1,0:T(8,128)(2,1)S(1)}, bf16[1,16,32,128]{3,2,1,0:T(8,128)(2,1)}, u32[]{:S(2)}) %copy-start.1) | copy-done | bytes 131096
  3.2 0.0 copy-start.2
  3.2 0.9 %copy-done.2 = bf16[1,16,32,128]{3,2,1,0:T(8,128)(2,1)S(1)} copy-done((bf16[1,16,32,128]{3,2,1,0:T(8,128)(2,1)S(1)}, bf16[1,16,32,128]{3,2,1,0:T(8,128)(2,1)}, u32[]{:S(2)}) %copy-start.2) | copy-done | bytes 131096
  4.1 51.3 %fields.1 = (f32[2,5,544,128]{3,2,1,0:T(8,128)S(1)}, f32[5,544,128]{2,1,0:T(8,128)}, f32[5,544,128]{2,1,0:T(8,128)}, f32[4,512,128]{2,1,0:T(8,128)}, f32[8,128]{1,0:T(8,128)S(1)}, /*index=5*/s32[1,1]{1,0:T(1,128)}) custom-call(s32[512,128]{1,0:T(8,128)S(1)} %bitcast.16, bf16[512,128]{1,0:T(8,128)(2,1)S(1)} %bitcast.17, bf16[512,128]{1,0:T(8,128)(2,1)S(1)} %bitcast.18, ...), custom_call_target="tpu_custom_call" | custom-call | tf_op jit(solution)/shard_map/fields/pallas_call | solution.py:826
  56.0 3.8 %conditional.1 = ((f32[512,512]{1,0:T(8,128)}, f32[512,512]{1,0:T(8,128)})) conditional(s32[]{:T(128)} %bitcast.5, (f32[2,5,544,128]{3,2,1,0:T(8,128)S(1)}, f32[512,512]{1,0:T(8,128)}) %tuple.13, (f32[2,5,544,128]{3,2,1,0:T(8,128)S(1)}, f32[5,544,128]{2,1,0:T(8,128)}, f32[5,544,128]{2,1,0:T(8,128)}, f32[4,512,128]{2,1,0:T(8,128)}, ...), branch_computations={%region_0.0_spmd, %region_1.0_spmd} | conditional | bytes 22347812 | solution.py:898
  56.2 3.6 %combine.1 = (f32[512,512]{1,0:T(8,128)}, f32[512,512]{1,0:T(8,128)}) custom-call(f32[2,5,544,128]{3,2,1,0:T(8,128)S(1)} %get-tuple-element.16.bw, f32[5,544,128]{2,1,0:T(8,128)} %get-tuple-element.17.first, f32[5,544,128]{2,1,0:T(8,128)} %get-tuple-element.18.second, f32[4,512,128]{2,1,0:T(8,128)} %get-tuple-element.19.third, ...), custom_call_target="tpu_custom_call" | custom-call | tf_op jit(solution)/shard_map/cond/branch_1_fun/combine/pallas_call | solution.py:880
  59.8 2.3 %copy.22 = f32[512,512]{1,0:T(8,128)} copy(f32[512,512]{1,0:T(8,128)} %get-tuple-element.53) | data formatting | bytes 2097152
  62.1 2.3 %copy.23 = f32[512,512]{1,0:T(8,128)} copy(f32[512,512]{1,0:T(8,128)} %get-tuple-element.54) | data formatting | bytes 2097152
Async XLA Ops:
  1.3 0.9 %copy-start = (s32[1,16,32,128]{3,2,1,0:T(8,128)S(1)}, s32[1,16,32,128]{3,2,1,0:T(8,128)}, u32[]{:S(2)}) copy-start(s32[1,16,32,128]{3,2,1,0:T(8,128)} %param.7) | copy-start | bytes 786436
  2.3 0.9 %copy-start.1 = (bf16[1,16,32,128]{3,2,1,0:T(8,128)(2,1)S(1)}, bf16[1,16,32,128]{3,2,1,0:T(8,128)(2,1)}, u32[]{:S(2)}) copy-start(bf16[1,16,32,128]{3,2,1,0:T(8,128)(2,1)} %param.8) | copy-start | bytes 393220
  3.2 0.9 %copy-start.2 = (bf16[1,16,32,128]{3,2,1,0:T(8,128)(2,1)S(1)}, bf16[1,16,32,128]{3,2,1,0:T(8,128)(2,1)}, u32[]{:S(2)}) copy-start(bf16[1,16,32,128]{3,2,1,0:T(8,128)(2,1)} %param.9) | copy-start | bytes 393220

commit v2 on v1

--- a/solution.py
+++ b/solution.py
@@ -17,6 +17,9 @@
 MARGIN = 16
 BAND = 16
 LIMIT = 2000.0
+FOLD = 64
+SPAN = TILE * (TILE // FOLD)
+ROOM = 59926118
 
 smooth_weight = 0.05
 
@@ -327,25 +330,29 @@
     return lax.div(value, size), lax.rem(value, size)
 
 
-def flip(place, code, size):
-    total, unit = 0, 1
-    while unit < size:
-        total = total + unit * lax.rem(place // unit + code // unit, 2)
-        unit *= 2
-    return total
+def digit_steps(place, size):
+    return [(1 << n) * (1 - 2 * lax.rem(place // (1 << n), 2)) for n in range(size.bit_length() - 1)]
+
+
+def flip(place, steps, code):
+    for n, step in enumerate(steps):
+        if code >> n & 1:
+            place = place + step
+    return place
 
 
 def field_kernel(
-    rows, cols, cell_hbm, value_hbm, weight_hbm, count_ref, kappa_hbm,
-    bw, first, second, third, coef, good,
-    cell_in, value_in, weight_in, cell_wide, value_wide, weight_wide,
+    rows, cols, cell_hbm, value_hbm, weight_hbm, count_hbm, kappa_hbm,
+    fields, coef, good,
+    cell_in, value_in, weight_in, count_in, cell_wide, value_wide, weight_wide,
     code_out, pair_out, code_out_inner, pair_out_inner,
     code_in, pair_in, code_in_inner, pair_in_inner,
     place_row, place_col, amounts, kap, mid,
     low_out, high_out, low_in, high_in, kap_low_out, kap_high_out, kap_low_in, kap_high_in,
     mine, sums,
-    load_sems, send_sem, recv_sems, halo_send, halo_recv, sum_send, sum_recv,
+    load_sems, send_sem, recv_sems, halo_send, halo_recv, sum_sems,
 ):
+    bw, first, second, third = fields.at[0:2], fields.at[2], fields.at[3], fields.at[4]
     count = rows * cols
     my_row, my_col = lax.axis_index("row"), lax.axis_index("col")
     me = my_row * cols + my_col
@@ -362,10 +369,11 @@
         pltpu.make_async_copy(cell_hbm, cell_in, load_sems.at[0]),
         pltpu.make_async_copy(value_hbm, value_in, load_sems.at[1]),
         pltpu.make_async_copy(weight_hbm, weight_in, load_sems.at[2]),
+        pltpu.make_async_copy(count_hbm, count_in, load_sems.at[3]),
     ]
     kappa_loads = [
         pltpu.make_async_copy(
-            kappa_hbm.at[:, pl.ds(c * LANES, LANES)], kap.at[c, pl.ds(MARGIN, height), :], load_sems.at[3 + c]
+            kappa_hbm.at[:, pl.ds(c * LANES, LANES)], kap.at[c, pl.ds(MARGIN, height), :], load_sems.at[4 + c]
         )
         for c in range(across)
     ]
@@ -379,7 +387,16 @@
         for field in (bw.at[0], bw.at[1], kap):
             field[c, 0:MARGIN, :] = strip
             field[c, bottom : bottom + MARGIN, :] = strip
-    greet_all(me, count, cols)
+
+    row_steps, col_steps = digit_steps(my_row, rows), digit_steps(my_col, cols)
+
+    def person(k):
+        return flip(my_row, row_steps, k % rows), flip(my_col, col_steps, k // rows)
+
+    barrier = pltpu.get_barrier_semaphore()
+    with jax.named_scope("greet"):
+        for k in reversed(range(1, count)):
+            pl.semaphore_signal(barrier, inc=1, device_id=person(k), device_id_type=MESH)
 
     for field in (bw.at[0], bw.at[1], kap):
         field[across, 0:MARGIN, :] = strip
@@ -389,12 +406,10 @@
             field[c, 0:8, :] = strip[:8]
             field[c, bottom + 8 : bottom + 16, :] = strip[:8]
 
-    def person(k):
-        code_col, code_row = k // rows, lax.rem(k, rows)
-        return flip(my_row, code_row, rows), flip(my_col, code_col, cols)
-
-    for load in loads:
-        load.wait()
+
+    with jax.named_scope("loads"):
+        for load in loads:
+            load.wait()
 
     def widen(t, carry):
         here = pl.ds(pl.multiple_of(t * count, 8), count)
@@ -405,8 +420,10 @@
         value_wide[there, :] = weight * value_in[here, :].astype(jnp.float32)
         return carry
 
-    lax.fori_loop(0, tiles, widen, 0)
-    dest_lane = lax.broadcasted_iota(jnp.int32, count_ref.shape, 1)
+    with jax.named_scope("widen"):
+        lax.fori_loop(0, tiles, widen, 0)
+    dest_lane = lax.broadcasted_iota(jnp.int32, count_in.shape, 1)
+    counts = count_in[...].astype(jnp.float32)
     slot_lane = lax.broadcasted_iota(jnp.int32, (tiles, slots), 1).astype(jnp.float32)
     edge_ids = [t for t in range(tiles) if t // across in (0, down - 1) or t % across in (0, across - 1)]
     inner_ids = [t for t in range(tiles) if t not in edge_ids]
@@ -421,14 +438,16 @@
             begin = end + 1
         return jnp.concatenate(parts, axis=0) if len(parts) > 1 else parts[0]
 
-    def encode(k, carry):
+    def encode(k):
         row, col = person(k)
         dest = row * cols + col
         every = pl.ds(dest, tiles, stride=pitch)
         cell = cell_wide[every, :]
         upper, _ = split(cell, width * cols)
-        local = split(upper, TILE)[1] * TILE + split(cell, TILE)[1]
-        alive = jnp.sum(jnp.where(dest_lane == dest, count_ref[...], 0.0), axis=1, keepdims=True)
+        line = split(upper, TILE)[1]
+        side, place = split(line, FOLD)
+        local = place * SPAN + side * TILE + split(cell, TILE)[1]
+        alive = jnp.sum(jnp.where(dest_lane == dest, counts, 0.0), axis=1, keepdims=True)
         local = jnp.where(slot_lane < alive, local, -1)
         weight, product = weight_wide[every, :], value_wide[every, :]
         code_out[k] = pick(local, edge_ids).astype(jnp.int16)
@@ -437,9 +456,10 @@
         pair_out_inner[k] = jnp.concatenate(
             [pick(weight, inner_ids), pick(product, inner_ids)], axis=0
         ).astype(jnp.bfloat16)
-        return carry
-
-    lax.fori_loop(0, count, encode, 0, unroll=2)
+
+    with jax.named_scope("encode"):
+        for k in reversed(range(count)):
+            encode(k)
     pieces = (
         ((code_out, code_in), (pair_out, pair_in), edges, edge_tile),
         ((code_out_inner, code_in_inner), (pair_out_inner, pair_in_inner), inners, inner_tile),
@@ -447,13 +467,14 @@
     for piece in pieces:
         for source, target in piece[:2]:
             target[0] = source[0]
-    await_all(count)
+    with jax.named_scope("arrive"):
+        await_all(count)
 
     bunch = GROUP
     chunks = count // bunch
 
     def send(piece, begin, end):
-        def one(k, carry):
+        for k in range(begin, end):
             place = person(k)
             for which, (source, target) in enumerate(pieces[piece][:2]):
                 pltpu.make_async_remote_copy(
@@ -461,15 +482,13 @@
                     send_sem=send_sem.at[piece, which], recv_sem=recv_sems.at[k // bunch, piece, which],
                     device_id=place, device_id_type=MESH,
                 ).start()
-            return carry
-
-        lax.fori_loop(begin, end, one, 0)
 
     half = count // 2
-    send(0, half, count)
-    send(0, 1, half)
-    send(1, 1, half)
-    send(1, half, count)
+    with jax.named_scope("send"):
+        send(0, half, count)
+        send(0, 1, half)
+        send(1, 1, half)
+        send(1, half, count)
 
     def halo_copies(group, body, parts):
         low_from, high_from, low_to, high_to = parts
@@ -553,37 +572,41 @@
     bw_halo = halo_copies(
         1, lambda part: bw.at[:, pl.ds(0, across), part, :], (low_out, high_out, low_in, high_in)
     )
-    for load in kappa_loads:
-        load.wait()
-    pack(kap, 0, kap_low_out, kap_high_out)
-    start_halo(kap_halo)
-
-    offsets = lax.broadcasted_iota(jnp.int32, (TILE, slots), 0).astype(jnp.float32).astype(jnp.bfloat16)
-    one = jnp.ones((TILE, slots), jnp.bfloat16)
-    zero = jnp.zeros((TILE, slots), jnp.bfloat16)
+    with jax.named_scope("kappa"):
+        for load in kappa_loads:
+            load.wait()
+        pack(kap, 0, kap_low_out, kap_high_out)
+        start_halo(kap_halo)
+
+    offsets = lax.broadcasted_iota(jnp.int32, (SPAN, slots), 0).astype(jnp.float32).astype(jnp.bfloat16)
+    one = jnp.ones((SPAN, slots), jnp.bfloat16)
+    zero = jnp.zeros((SPAN, slots), jnp.bfloat16)
 
     def bin_chunk(chunk, piece):
         codes, pairs, some, locate = pieces[piece]
         for which, (_, target) in enumerate((codes, pairs)):
             begin = chunk * bunch + (1 if chunk == 0 else 0)
             part = target.at[pl.ds(begin, (chunk + 1) * bunch - begin)]
-            pltpu.make_async_copy(part, part, recv_sems.at[chunk, piece, which]).wait()
-        for n in range(bunch):
-            code = codes[1][chunk * bunch + n].astype(jnp.int32)
-            place_row[n * some : (n + 1) * some, :] = (code >> 7).astype(jnp.float32)
-            place_col[n * some : (n + 1) * some, :] = (code & (TILE - 1)).astype(jnp.float32)
-            amounts[n * 2 * some : (n + 1) * 2 * some, :] = pairs[1][chunk * bunch + n].astype(jnp.float32)
-
-        def spread(ref, at):
-            return jnp.broadcast_to(ref[pl.ds(at, 1), :].astype(jnp.bfloat16), (TILE, slots))
+            with jax.named_scope(f"wait{piece}"):
+                pltpu.make_async_copy(part, part, recv_sems.at[chunk, piece, which]).wait()
+        with jax.named_scope("spread"):
+            for n in range(bunch):
+                code = codes[1][chunk * bunch + n].astype(jnp.int32)
+                place_row[n * some : (n + 1) * some, :] = (code >> (SPAN.bit_length() - 1)).astype(jnp.float32)
+                place_col[n * some : (n + 1) * some, :] = (code & (SPAN - 1)).astype(jnp.float32)
+                amounts[n * 2 * some : (n + 1) * 2 * some, :] = pairs[1][chunk * bunch + n].astype(jnp.float32)
+
+        def spread(ref, at, size):
+            return jnp.broadcast_to(ref[pl.ds(at, 1), :].astype(jnp.bfloat16), (size, slots))
 
         def bin_tile(e, carry):
             hot, weights, products = [], [], []
             for n in range(bunch):
-                hot.append(jnp.where(spread(place_col, n * some + e) == offsets, one, zero))
-                hit = spread(place_row, n * some + e) == offsets
-                weights.append(jnp.where(hit, spread(amounts, n * 2 * some + e), zero))
-                products.append(jnp.where(hit, spread(amounts, n * 2 * some + some + e), zero))
+                hit = spread(place_col, n * some + e, SPAN) == offsets
+                hot.append(jnp.where(hit, one, zero).astype(jnp.float8_e4m3fn))
+                hit = spread(place_row, n * some + e, FOLD) == offsets[:FOLD]
+                weights.append(jnp.where(hit, spread(amounts, n * 2 * some + e, FOLD), zero[:FOLD]))
+                products.append(jnp.where(hit, spread(amounts, n * 2 * some + some + e, FOLD), zero[:FOLD]))
             stacked = jnp.concatenate(
                 [jnp.concatenate(products, axis=1), jnp.concatenate(weights, axis=1)], axis=0
             )
@@ -592,36 +615,52 @@
                 preferred_element_type=jnp.float32,
             )
             row, col = locate(e, down, across)
-            here = pl.ds(pl.multiple_of(MARGIN + row * TILE, 8), TILE)
-            if chunk == 0:
-                bw[0, col, here, :] = total[:TILE]
-                bw[1, col, here, :] = total[TILE:]
-            else:
-                bw[0, col, here, :] += total[:TILE]
-                bw[1, col, here, :] += total[TILE:]
+            for n in range(TILE // FOLD):
+                here = pl.ds(pl.multiple_of(MARGIN + row * TILE + n * FOLD, 8), FOLD)
+                lanes = slice(n * TILE, (n + 1) * TILE)
+                for which in range(2):
+                    part = total[which * FOLD : (which + 1) * FOLD, lanes]
+                    if chunk == 0:
+                        bw[which, col, here, :] = part
+                    else:
+                        bw[which, col, here, :] += part
             return carry
 
-        lax.fori_loop(0, some, bin_tile, 0, unroll=4)
+        with jax.named_scope("bin"):
+            lax.fori_loop(0, some, bin_tile, 0, unroll=4)
 
     for chunk in range(chunks // 2):
         bin_chunk(chunk, 0)
         bin_chunk(chunk, 1)
     for chunk in range(chunks // 2, chunks):
         bin_chunk(chunk, 0)
-    for which in range(2):
-        pack(bw.at[which], 8 * which, low_out, high_out)
-    start_halo(bw_halo)
+    with jax.named_scope("pack"):
+        for which in range(2):
+            pack(bw.at[which], 8 * which, low_out, high_out)
+        start_halo(bw_halo)
     for chunk in range(chunks // 2, chunks):
         bin_chunk(chunk, 1)
-    end_halo(kap_halo)
-    unpack(kap, 0, kap_low_in, kap_high_in)
-    for piece in range(2):
-        for which, (source, _) in enumerate(pieces[piece][:2]):
-            part = source.at[pl.ds(1, count - 1)]
-            pltpu.make_async_copy(part, part, send_sem.at[piece, which]).wait()
-    end_halo(bw_halo)
-    for which in range(2):
-        unpack(bw.at[which], 8 * which, low_in, high_in)
+    with jax.named_scope("kap_halo"):
+        end_halo(kap_halo)
+        unpack(kap, 0, kap_low_in, kap_high_in)
+
+        def lift(i, carry):
+            here = pl.ds(pl.multiple_of(i * 16, 8), 16)
+            for c in range(across + 1):
+                kap[c, here, :] = 4.0 + kap[c, here, :]
+            return carry
+
+        lax.fori_loop(0, kap.shape[1] // 16, lift, 0, unroll=2)
+    with jax.named_scope("sent"):
+        for piece in range(2):
+            for which, (source, _) in enumerate(pieces[piece][:2]):
+                part = source.at[pl.ds(1, count - 1)]
+                pltpu.make_async_copy(part, part, send_sem.at[piece, which]).wait()
+    with jax.named_scope("halo"):
+        end_halo(bw_halo)
+    with jax.named_scope("unpack"):
+        for which in range(2):
+            unpack(bw.at[which], 8 * which, low_in, high_in)
 
     up, under = my_row > 0, my_row < rows - 1
     live = ((lane < 8) & (my_col < cols - 1)) | ((lane >= LANES - 8) & (my_col > 0))
@@ -637,7 +676,7 @@
             beside = field[c, pl.ds(at - 1, size), :] + field[c, pl.ds(at + 1, size), :]
             beside = beside + jnp.where(lane == 0, ahead[c - 1], ahead[c])
             beside = beside + jnp.where(lane == LANES - 1, behind[(c + 1) % (across + 1)], behind[c])
-            value = (4.0 + kap[c, here, :]) * center[c] - beside
+            value = kap[c, here, :] * center[c] - beside
             result.append(jnp.where(live, value, 0.0) if c == across else value)
         return result
 
@@ -648,7 +687,7 @@
         def step(i, carry):
             return body(pl.multiple_of(MARGIN + i * BAND, 8), carry)
 
-        return lax.fori_loop(0, height // BAND, step, carry)
+        return lax.fori_loop(0, height // BAND, step, carry, unroll=8)
 
     def fold(value):
         total = value[0:8]
@@ -692,48 +731,48 @@
             store(at, 8, there)
 
     moments = []
-    moments += apply_inner(response)
-    apply_outer(response, first)
-    moments += apply_inner(first)
-    apply_outer(first, second)
-    moments += apply_inner(second)
-
-    both = jnp.zeros((1, LANES), jnp.float32)
-    for at, value in enumerate(moments):
-        total = jnp.sum(jnp.sum(value, axis=0, keepdims=True), axis=1, keepdims=True)
-        both = jnp.where(lane == at, total, both)
-    mine[...] = both
-    sums[me] = both
-
-    def sum_copy(k, slot):
-        return pltpu.make_async_remote_copy(
-            src_ref=mine, dst_ref=sums.at[slot],
-            send_sem=sum_send.at[k], recv_sem=sum_recv.at[k],
-            device_id=person(k), device_id_type=MESH,
-        )
-
-    def begin(i, carry):
-        sum_copy(count - 1 - i, me).start()
-        return carry
-
-    lax.fori_loop(0, count - 1, begin, 0)
+    with jax.named_scope("op1"):
+        moments += apply_inner(response)
+    with jax.named_scope("op2"):
+        apply_outer(response, first)
+    with jax.named_scope("op3"):
+        moments += apply_inner(first)
+    with jax.named_scope("op4"):
+        apply_outer(first, second)
+    with jax.named_scope("op5"):
+        moments += apply_inner(second)
+
+    with jax.named_scope("fold"):
+        both = jnp.zeros((1, LANES), jnp.float32)
+        for at, value in enumerate(moments):
+            total = jnp.sum(jnp.sum(value, axis=0, keepdims=True), axis=1, keepdims=True)
+            both = jnp.where(lane == at, total, both)
+        mine[...] = both
+        sums[me] = both
+
+    with jax.named_scope("sum_send"):
+        for k in reversed(range(1, count)):
+            pltpu.make_async_remote_copy(
+                src_ref=mine, dst_ref=sums.at[me],
+                send_sem=sum_sems.at[0], recv_sem=sum_sems.at[1],
+                device_id=person(k), device_id_type=MESH,
+            ).start()
 
     def last(at, carry):
         for c, value in enumerate(inner(mid, at, BAND, across)):
             here = pl.ds(at, BAND)
-            third[c, pl.ds(pl.multiple_of(at - MARGIN, 8), BAND), :] = (
-                weight[c, here, :] * second[c, here, :] + smooth_weight * value
-            )
+            third[c, here, :] = weight[c, here, :] * second[c, here, :] + smooth_weight * value
         return carry
 
-    bands(last, 0)
-
-    def finish(k, carry):
-        row, col = person(k)
-        sum_copy(k, row * cols + col).wait()
-        return carry
-
-    lax.fori_loop(1, count, finish, 0)
+    with jax.named_scope("op6"):
+        bands(last, 0)
+
+    with jax.named_scope("sum_wait"):
+        part = sums.at[pl.ds(1, count - 1)]
+        for n in range(2):
+            pltpu.make_async_copy(part, part, sum_sems.at[n]).wait()
+    coef_scope = jax.named_scope("coef")
+    coef_scope.__enter__()
     total = jnp.sum(sums[...], axis=0)
     m = [jnp.sum(jnp.where(lane == at, total, 0.0), axis=1, keepdims=True) for at in range(6)]
     scale = m[1] / m[0]
@@ -769,10 +808,12 @@
     sound = sound & (lead * LIMIT >= lead_size) & (turn * LIMIT >= turn_size)
     sound = sound & (alpha * lead * (2.0 * LIMIT) >= 1.0 + a * a * n[2] + alpha * alpha * n[4])
     good[...] = jnp.where(sound, 1, 0)
-
-
-def combine_kernel(bw, first, second, third, coef, x_hbm, r_hbm, x_out, r_out, sems):
-    across, height, _ = third.shape
+    coef_scope.__exit__(None, None, None)
+
+
+def combine_kernel(fields, coef, x_hbm, r_hbm, x_out, r_out, sems):
+    height, width = x_hbm.shape
+    across = width // LANES
     band = height // 8
     weights = [coef[at : at + 1, :] for at in range(6)]
     copies = []
@@ -783,7 +824,7 @@
             at = pl.multiple_of(i * band + j * 32, 8)
             for c in range(across):
                 here = pl.ds(MARGIN + at, 32)
-                values = [bw[0, c, here, :], first[c, here, :], second[c, here, :], third[c, pl.ds(at, 32), :]]
+                values = [fields[n, c, here, :] for n in (0, 2, 3, 4)]
                 lanes = slice(c * LANES, (c + 1) * LANES)
                 x_out[pl.ds(at, 32), lanes] = (
                     weights[0] * values[0] + weights[1] * values[1] + weights[2] * values[2]
@@ -802,6 +843,11 @@
         copy.wait()
 
 
+def copy_kernel(x_in, r_in, x_out, r_out):
+    x_out[...] = x_in[...]
+    r_out[...] = r_in[...]
+
+
 def per_device(rows, cols, obs_cell, obs_value, obs_weight, obs_count, kappa_field):
     count = rows * cols
     height, width = kappa_field.shape
@@ -809,7 +855,6 @@
     down, across = height // TILE, width // TILE
     edges, inners = edge_and_inner(down, across)
     in_vmem = pl.BlockSpec(memory_space=pltpu.VMEM)
-    anywhere = pl.BlockSpec(memory_space=pl.ANY)
     in_hbm = pl.BlockSpec(memory_space=pltpu.HBM)
     tall = height + 2 * MARGIN
     field = jax.ShapeDtypeStruct((height, width), jnp.float32)
@@ -823,22 +868,20 @@
         pltpu.VMEM((count, inners, slots), jnp.int16),
         pltpu.VMEM((count, 2 * inners, slots), jnp.bfloat16),
     ]
-    bw, first, second, third, coef, good = pl.pallas_call(
+    fields, coef, good = pl.pallas_call(
         functools.partial(field_kernel, rows, cols),
         out_shape=(
-            jax.ShapeDtypeStruct((2, across + 1, tall, LANES), jnp.float32),
-            wide,
-            wide,
-            jax.ShapeDtypeStruct((across, height, LANES), jnp.float32),
+            jax.ShapeDtypeStruct((5, across + 1, tall, LANES), jnp.float32),
             jax.ShapeDtypeStruct((8, LANES), jnp.float32),
             jax.ShapeDtypeStruct((1, 1), jnp.int32),
         ),
-        in_specs=[anywhere] * 3 + [in_vmem, anywhere],
-        out_specs=(in_vmem,) * 6,
+        in_specs=[in_hbm] * 5,
+        out_specs=(in_vmem,) * 3,
         scratch_shapes=[
             pltpu.VMEM(flat, jnp.int32),
             pltpu.VMEM(flat, jnp.bfloat16),
             pltpu.VMEM(flat, jnp.bfloat16),
+            pltpu.VMEM((tiles, count), jnp.int32),
             pltpu.VMEM(pitched, jnp.int32),
             pltpu.VMEM(pitched, jnp.float32),
             pltpu.VMEM(pitched, jnp.float32),
@@ -859,28 +902,27 @@
             pltpu.VMEM((8, height + 2 * LANES), jnp.float32),
             pltpu.VMEM((1, LANES), jnp.float32),
             pltpu.VMEM((count, 1, LANES), jnp.float32),
-            pltpu.SemaphoreType.DMA((3 + across,)),
+            pltpu.SemaphoreType.DMA((4 + across,)),
             pltpu.SemaphoreType.DMA((2, 2)),
             pltpu.SemaphoreType.DMA((count // GROUP, 2, 2)),
             pltpu.SemaphoreType.DMA((2, 8)),
             pltpu.SemaphoreType.DMA((2, 8)),
-            pltpu.SemaphoreType.DMA((count,)),
-            pltpu.SemaphoreType.DMA((count,)),
+            pltpu.SemaphoreType.DMA((2,)),
         ],
         compiler_params=pltpu.CompilerParams(
-            collective_id=0, has_side_effects=True, vmem_limit_bytes=30 << 20
+            collective_id=0, has_side_effects=True, vmem_limit_bytes=ROOM
         ),
         name="fields",
     )(
         obs_cell.reshape(flat), obs_value.reshape(flat), obs_weight.reshape(flat),
-        obs_count[0].astype(jnp.float32), kappa_field,
+        obs_count[0], kappa_field,
     )
 
-    def combine(bw, first, second, third, coef, kappa):
+    def combine(fields, coef, *unused):
         return pl.pallas_call(
             combine_kernel,
             out_shape=(field, field),
-            in_specs=[in_vmem] * 5,
+            in_specs=[in_vmem] * 2,
             out_specs=(in_hbm,) * 2,
             scratch_shapes=[
                 pltpu.VMEM(field.shape, jnp.float32),
@@ -889,13 +931,19 @@
             ],
             compiler_params=pltpu.CompilerParams(vmem_limit_bytes=16 << 20),
             name="combine",
-        )(bw, first, second, third, coef)
-
-    def iterate(bw, first, second, third, coef, kappa):
-        own = bw[:, :across, MARGIN : MARGIN + height, :].transpose(0, 2, 1, 3).reshape(2, height, width)
-        return smooth(rows, cols, own[0], own[1], kappa)
-
-    return lax.cond(good[0, 0] > 0, combine, iterate, bw, first, second, third, coef, kappa_field)
+        )(fields, coef)
+
+    def iterate(fields, coef, kappa):
+        own = fields[:2, :across, MARGIN : MARGIN + height, :].transpose(0, 2, 1, 3).reshape(2, height, width)
+        return pl.pallas_call(
+            copy_kernel,
+            out_shape=(field, field),
+            in_specs=[in_vmem] * 2,
+            out_specs=(in_vmem,) * 2,
+            name="hand_on",
+        )(*smooth(rows, cols, own[0], own[1], kappa))
+
+    return lax.cond(good[0, 0] > 0, combine, iterate, fields, coef, kappa_field)
 
 
 def smooth(rows, cols, response, weight_field, kappa_field):

time: 64.7 us -> 38.7 us (0.60)
  Pallas kernels: 54.9 us -> 36.9 us
  local copies, waits for them, and re-layouts: 7.28 us -> 0 us
  other arithmetic: 0.7 us -> 0 us
    pallas_call x1, Pallas kernels: 51.3 us -> 35.4 us  [per_device(): pl.pallas_call(functools.partial(field_kernel, rows, cols), out_shape=(ja...]
    unnamed x8 -> x0, local copies, waits for them, and re-layouts: 7.28 us -> none
    pallas_call x1, Pallas kernels: 3.6 us -> 1.49 us  [combine(): pl.pallas_call(combine_kernel, out_shape=(field, field), in_specs=[in_vme...]
    convert_element_type x1 -> x0, other arithmetic: 0.7 us -> none  [per_device(): obs_count[0].astype(jnp.float32)]
where the time goes in v2:
time: 38.7 us; the launch traced here: 38.6 us
  Pallas kernels  36.9 us (95%)
  between operations  1.43 us (4%)
    pallas_call x1, Pallas kernels, per_device(): pl.pallas_call(functools.partial(field_kernel, rows, cols), out_shape=(ja...  35.4 us
    pallas_call x1, Pallas kernels, combine(): pl.pallas_call(combine_kernel, out_shape=(field, field), in_specs=[in_vme...  1.49 us

profile of v2, /device:TPU:0, one launch (start us, length us, event | category | flops | bytes accessed | tf_op | source)
XLA Modules:
  0.0 38.6 jit_solution(11348054659353394384)
XLA Ops:
  0.6 35.4 %fields.1 = (f32[5,5,544,128]{3,2,1,0:T(8,128)S(1)}, f32[8,128]{1,0:T(8,128)S(1)}, s32[1,1]{1,0:T(1,128)}) custom-call(s32[512,128]{1,0:T(8,128)} %bitcast.17, bf16[512,128]{1,0:T(8,128)(2,1)} %bitcast.18, bf16[512,128]{1,0:T(8,128)(2,1)} %bitcast.19, s32[16,32]{1,0:T(8,128)} %bitcast.20, f32[512,512]{1,0:T(8,128)} %kappa_hbm.1), custom_call_target="tpu_custom_call" | custom-call | tf_op jit(solution)/shard_map/fields/pallas_call | solution.py:871
  36.7 1.7 %conditional.1 = ((f32[512,512]{1,0:T(8,128)}, f32[512,512]{1,0:T(8,128)})) conditional(s32[]{:T(128)} %bitcast.5, (f32[5,5,544,128]{3,2,1,0:T(8,128)S(1)}, f32[512,512]{1,0:T(8,128)}) %tuple.13, (f32[5,5,544,128]{3,2,1,0:T(8,128)S(1)}, f32[8,128]{1,0:T(8,128)S(1)}) %tuple.14), branch_computations={%region_0.0_spmd, %region_1.0_spmd} | conditional | bytes 39092316 | solution.py:946
  36.9 1.5 %combine.1 = (f32[512,512]{1,0:T(8,128)}, f32[512,512]{1,0:T(8,128)}) custom-call(f32[5,5,544,128]{3,2,1,0:T(8,128)S(1)} %get-tuple-element.12.fields, f32[8,128]{1,0:T(8,128)S(1)} %get-tuple-element.13.coef), custom_call_target="tpu_custom_call" | custom-call | tf_op jit(solution)/shard_map/cond/branch_1_fun/combine/pallas_call | solution.py:922

commit v3 on v2

--- a/solution.py
+++ b/solution.py
@@ -16,7 +16,9 @@
 LANES = 128
 MARGIN = 16
 BAND = 16
-LIMIT = 2000.0
+LIMIT = 1000.0
+UNROLL = 32
+TILES_AT_ONCE = 4
 FOLD = 64
 SPAN = TILE * (TILE // FOLD)
 ROOM = 59926118
@@ -307,6 +309,11 @@
         lax.fori_loop(0, height // 32, advance, 0)
 
 
+def cuts_of(count):
+    cuts = list(range(0, count, GROUP)) + [count]
+    return cuts[:-1] + [count - GROUP // 2, count]
+
+
 def edge_and_inner(down, across):
     edge = 2 * across + 2 * (down - 2)
     return edge, (down - 2) * (across - 2)
@@ -343,10 +350,9 @@
 
 def field_kernel(
     rows, cols, cell_hbm, value_hbm, weight_hbm, count_hbm, kappa_hbm,
-    fields, coef, good,
+    fields, coef,
     cell_in, value_in, weight_in, count_in, cell_wide, value_wide, weight_wide,
-    code_out, pair_out, code_out_inner, pair_out_inner,
-    code_in, pair_in, code_in_inner, pair_in_inner,
+    code_out, pair_out, code_in, pair_in,
     place_row, place_col, amounts, kap, mid,
     low_out, high_out, low_in, high_in, kap_low_out, kap_high_out, kap_low_in, kap_high_in,
     mine, sums,
@@ -389,9 +395,10 @@
             field[c, bottom : bottom + MARGIN, :] = strip
 
     row_steps, col_steps = digit_steps(my_row, rows), digit_steps(my_col, cols)
+    col_codes = list(range(cols))
 
     def person(k):
-        return flip(my_row, row_steps, k % rows), flip(my_col, col_steps, k // rows)
+        return flip(my_row, row_steps, k % rows), flip(my_col, col_steps, col_codes[k // rows])
 
     barrier = pltpu.get_barrier_semaphore()
     with jax.named_scope("greet"):
@@ -425,19 +432,6 @@
     dest_lane = lax.broadcasted_iota(jnp.int32, count_in.shape, 1)
     counts = count_in[...].astype(jnp.float32)
     slot_lane = lax.broadcasted_iota(jnp.int32, (tiles, slots), 1).astype(jnp.float32)
-    edge_ids = [t for t in range(tiles) if t // across in (0, down - 1) or t % across in (0, across - 1)]
-    inner_ids = [t for t in range(tiles) if t not in edge_ids]
-
-    def pick(value, ids):
-        parts, begin = [], 0
-        while begin < len(ids):
-            end = begin
-            while end + 1 < len(ids) and ids[end + 1] == ids[end] + 1:
-                end += 1
-            parts.append(value[ids[begin] : ids[end] + 1])
-            begin = end + 1
-        return jnp.concatenate(parts, axis=0) if len(parts) > 1 else parts[0]
-
     def encode(k):
         row, col = person(k)
         dest = row * cols + col
@@ -450,45 +444,30 @@
         alive = jnp.sum(jnp.where(dest_lane == dest, counts, 0.0), axis=1, keepdims=True)
         local = jnp.where(slot_lane < alive, local, -1)
         weight, product = weight_wide[every, :], value_wide[every, :]
-        code_out[k] = pick(local, edge_ids).astype(jnp.int16)
-        pair_out[k] = jnp.concatenate([pick(weight, edge_ids), pick(product, edge_ids)], axis=0).astype(jnp.bfloat16)
-        code_out_inner[k] = pick(local, inner_ids).astype(jnp.int16)
-        pair_out_inner[k] = jnp.concatenate(
-            [pick(weight, inner_ids), pick(product, inner_ids)], axis=0
-        ).astype(jnp.bfloat16)
+        code_out[k] = local.astype(jnp.int16)
+        pair_out[k] = jnp.concatenate([weight, product], axis=0).astype(jnp.bfloat16)
 
     with jax.named_scope("encode"):
         for k in reversed(range(count)):
             encode(k)
-    pieces = (
-        ((code_out, code_in), (pair_out, pair_in), edges, edge_tile),
-        ((code_out_inner, code_in_inner), (pair_out_inner, pair_in_inner), inners, inner_tile),
-    )
-    for piece in pieces:
-        for source, target in piece[:2]:
-            target[0] = source[0]
+    buffers = ((code_out, code_in), (pair_out, pair_in))
+    for source, target in buffers:
+        target[0] = source[0]
     with jax.named_scope("arrive"):
         await_all(count)
 
-    bunch = GROUP
-    chunks = count // bunch
-
-    def send(piece, begin, end):
-        for k in range(begin, end):
+    cuts = cuts_of(count)
+    chunks = len(cuts) - 1
+
+    with jax.named_scope("send"):
+        for k in range(1, count):
             place = person(k)
-            for which, (source, target) in enumerate(pieces[piece][:2]):
+            for which, (source, target) in enumerate(buffers):
                 pltpu.make_async_remote_copy(
                     src_ref=source.at[k], dst_ref=target.at[k],
-                    send_sem=send_sem.at[piece, which], recv_sem=recv_sems.at[k // bunch, piece, which],
+                    send_sem=send_sem.at[which], recv_sem=recv_sems.at[sum(k >= cut for cut in cuts[1:]), which],
                     device_id=place, device_id_type=MESH,
                 ).start()
-
-    half = count // 2
-    with jax.named_scope("send"):
-        send(0, half, count)
-        send(0, 1, half)
-        send(1, 1, half)
-        send(1, half, count)
 
     def halo_copies(group, body, parts):
         low_from, high_from, low_to, high_to = parts
@@ -550,8 +529,9 @@
         for j in range(down):
             here = pl.ds(MARGIN + j * TILE, TILE)
             there = slice(j * TILE, (j + 1) * TILE)
-            low[at : at + 8, there] = field[0, here, :].T[:8]
-            high[at : at + 8, there] = field[across - 1, here, :].T[TILE - 8 :]
+            sides = jnp.where(lane < LANES // 2, field[0, here, :], field[across - 1, here, :]).T
+            low[at : at + 8, there] = sides[:8]
+            high[at : at + 8, there] = sides[TILE - 8 :]
 
     gap = jnp.zeros((LANES - 16, LANES), jnp.float32)
 
@@ -582,31 +562,33 @@
     one = jnp.ones((SPAN, slots), jnp.bfloat16)
     zero = jnp.zeros((SPAN, slots), jnp.bfloat16)
 
-    def bin_chunk(chunk, piece):
-        codes, pairs, some, locate = pieces[piece]
-        for which, (_, target) in enumerate((codes, pairs)):
-            begin = chunk * bunch + (1 if chunk == 0 else 0)
-            part = target.at[pl.ds(begin, (chunk + 1) * bunch - begin)]
-            with jax.named_scope(f"wait{piece}"):
-                pltpu.make_async_copy(part, part, recv_sems.at[chunk, piece, which]).wait()
+    def take_chunk(chunk):
+        begin, end = max(cuts[chunk], 1), cuts[chunk + 1]
+        with jax.named_scope("wait"):
+            for which, (_, target) in enumerate(buffers):
+                part = target.at[pl.ds(begin, end - begin)]
+                pltpu.make_async_copy(part, part, recv_sems.at[chunk, which]).wait()
         with jax.named_scope("spread"):
-            for n in range(bunch):
-                code = codes[1][chunk * bunch + n].astype(jnp.int32)
-                place_row[n * some : (n + 1) * some, :] = (code >> (SPAN.bit_length() - 1)).astype(jnp.float32)
-                place_col[n * some : (n + 1) * some, :] = (code & (SPAN - 1)).astype(jnp.float32)
-                amounts[n * 2 * some : (n + 1) * 2 * some, :] = pairs[1][chunk * bunch + n].astype(jnp.float32)
-
+            for n in range(cuts[chunk], end):
+                code = code_in[n].astype(jnp.int32)
+                place_row[n * tiles : (n + 1) * tiles, :] = (code >> (SPAN.bit_length() - 1)).astype(jnp.float32)
+                place_col[n * tiles : (n + 1) * tiles, :] = (code & (SPAN - 1)).astype(jnp.float32)
+                amounts[n * 2 * tiles : (n + 1) * 2 * tiles, :] = pair_in[n].astype(jnp.float32)
+
+    def bin_chunk(begin, end, some, locate):
         def spread(ref, at, size):
             return jnp.broadcast_to(ref[pl.ds(at, 1), :].astype(jnp.bfloat16), (size, slots))
 
         def bin_tile(e, carry):
             hot, weights, products = [], [], []
-            for n in range(bunch):
-                hit = spread(place_col, n * some + e, SPAN) == offsets
+            row, col = locate(e, down, across)
+            tile = row * across + col
+            for n in range(begin, end):
+                hit = spread(place_col, n * tiles + tile, SPAN) == offsets
                 hot.append(jnp.where(hit, one, zero).astype(jnp.float8_e4m3fn))
-                hit = spread(place_row, n * some + e, FOLD) == offsets[:FOLD]
-                weights.append(jnp.where(hit, spread(amounts, n * 2 * some + e, FOLD), zero[:FOLD]))
-                products.append(jnp.where(hit, spread(amounts, n * 2 * some + some + e, FOLD), zero[:FOLD]))
+                hit = spread(place_row, n * tiles + tile, FOLD) == offsets[:FOLD]
+                weights.append(jnp.where(hit, spread(amounts, n * 2 * tiles + tile, FOLD), zero[:FOLD]))
+                products.append(jnp.where(hit, spread(amounts, (n * 2 + 1) * tiles + tile, FOLD), zero[:FOLD]))
             stacked = jnp.concatenate(
                 [jnp.concatenate(products, axis=1), jnp.concatenate(weights, axis=1)], axis=0
             )
@@ -614,32 +596,29 @@
                 stacked, jnp.concatenate(hot, axis=1), (((1,), (1,)), ((), ())),
                 preferred_element_type=jnp.float32,
             )
-            row, col = locate(e, down, across)
             for n in range(TILE // FOLD):
                 here = pl.ds(pl.multiple_of(MARGIN + row * TILE + n * FOLD, 8), FOLD)
                 lanes = slice(n * TILE, (n + 1) * TILE)
                 for which in range(2):
                     part = total[which * FOLD : (which + 1) * FOLD, lanes]
-                    if chunk == 0:
+                    if begin == 0:
                         bw[which, col, here, :] = part
                     else:
                         bw[which, col, here, :] += part
             return carry
 
         with jax.named_scope("bin"):
-            lax.fori_loop(0, some, bin_tile, 0, unroll=4)
-
-    for chunk in range(chunks // 2):
-        bin_chunk(chunk, 0)
-        bin_chunk(chunk, 1)
-    for chunk in range(chunks // 2, chunks):
-        bin_chunk(chunk, 0)
+            lax.fori_loop(0, some, bin_tile, 0, unroll=TILES_AT_ONCE)
+
+    for chunk in range(chunks):
+        take_chunk(chunk)
+        bin_chunk(cuts[chunk], cuts[chunk + 1], edges, edge_tile)
     with jax.named_scope("pack"):
         for which in range(2):
             pack(bw.at[which], 8 * which, low_out, high_out)
         start_halo(bw_halo)
-    for chunk in range(chunks // 2, chunks):
-        bin_chunk(chunk, 1)
+    for begin in range(0, count, GROUP):
+        bin_chunk(begin, begin + GROUP, inners, inner_tile)
     with jax.named_scope("kap_halo"):
         end_halo(kap_halo)
         unpack(kap, 0, kap_low_in, kap_high_in)
@@ -652,10 +631,9 @@
 
         lax.fori_loop(0, kap.shape[1] // 16, lift, 0, unroll=2)
     with jax.named_scope("sent"):
-        for piece in range(2):
-            for which, (source, _) in enumerate(pieces[piece][:2]):
-                part = source.at[pl.ds(1, count - 1)]
-                pltpu.make_async_copy(part, part, send_sem.at[piece, which]).wait()
+        for which, (source, _) in enumerate(buffers):
+            part = source.at[pl.ds(1, count - 1)]
+            pltpu.make_async_copy(part, part, send_sem.at[which]).wait()
     with jax.named_scope("halo"):
         end_halo(bw_halo)
     with jax.named_scope("unpack"):
@@ -687,7 +665,7 @@
         def step(i, carry):
             return body(pl.multiple_of(MARGIN + i * BAND, 8), carry)
 
-        return lax.fori_loop(0, height // BAND, step, carry, unroll=8)
+        return lax.fori_loop(0, height // BAND, step, carry, unroll=UNROLL)
 
     def fold(value):
         total = value[0:8]
@@ -695,52 +673,60 @@
             total = total + value[n : n + 8]
         return total
 
-    def apply_inner(source):
+    blank = jnp.zeros((8, LANES), jnp.float32)
+
+    def apply_inner(source, measure=False):
         def body(at, carry):
-            square, energy = carry
             for c, value in enumerate(inner(source, at, BAND, across + 1)):
                 here = pl.ds(at, BAND)
                 mid[c, here, :] = value
-                if c < across:
+                if measure and c < across:
+                    square, energy = carry
                     x = source[c, here, :]
                     xx = x * x
                     square = square + fold(xx)
                     energy = energy + fold(weight[c, here, :] * xx + smooth_weight * (value * value))
-            return square, energy
-
-        blank = jnp.zeros((8, LANES), jnp.float32)
-        result = bands(body, (blank, blank))
+                    carry = square, energy
+            return carry
+
+        result = bands(body, (blank, blank) if measure else 0)
         for at, there in outer:
             for c, value in enumerate(inner(source, at, 8, across + 1)):
                 mid[c, pl.ds(at, 8), :] = jnp.where(there, value, 0.0)
         return result
 
     def apply_outer(source, target):
-        def store(at, size, there=None):
-            for c, value in enumerate(inner(mid, at, size, across + 1)):
-                here = pl.ds(at, size)
+        def body(at, carry):
+            square, energy = carry
+            for c, value in enumerate(inner(mid, at, BAND, across + 1)):
+                here = pl.ds(at, BAND)
+                x = source[c, here, :]
+                value = weight[c, here, :] * x + smooth_weight * value
+                target[c, here, :] = value
+                if c < across:
+                    square = square + fold(x * x)
+                    energy = energy + fold(x * value)
+            return square, energy
+
+        result = bands(body, (blank, blank))
+        for at, there in outer:
+            for c, value in enumerate(inner(mid, at, 8, across + 1)):
+                here = pl.ds(at, 8)
                 value = weight[c, here, :] * source[c, here, :] + smooth_weight * value
-                target[c, here, :] = value if there is None else jnp.where(there, value, 0.0)
-
-        def body(at, carry):
-            store(at, BAND)
-            return carry
-
-        bands(body, 0)
-        for at, there in outer:
-            store(at, 8, there)
+                target[c, here, :] = jnp.where(there, value, 0.0)
+        return result
 
     moments = []
     with jax.named_scope("op1"):
-        moments += apply_inner(response)
+        apply_inner(response)
     with jax.named_scope("op2"):
-        apply_outer(response, first)
+        moments += apply_outer(response, first)
     with jax.named_scope("op3"):
-        moments += apply_inner(first)
+        apply_inner(first)
     with jax.named_scope("op4"):
-        apply_outer(first, second)
+        moments += apply_outer(first, second)
     with jax.named_scope("op5"):
-        moments += apply_inner(second)
+        moments += apply_inner(second, True)
 
     with jax.named_scope("fold"):
         both = jnp.zeros((1, LANES), jnp.float32)
@@ -773,7 +759,10 @@
             pltpu.make_async_copy(part, part, sum_sems.at[n]).wait()
     coef_scope = jax.named_scope("coef")
     coef_scope.__enter__()
-    total = jnp.sum(sums[...], axis=0)
+    total = [sums[n] for n in range(count)]
+    while len(total) > 1:
+        total = [total[n] + total[n + 1] for n in range(0, len(total), 2)]
+    total = total[0]
     m = [jnp.sum(jnp.where(lane == at, total, 0.0), axis=1, keepdims=True) for at in range(6)]
     scale = m[1] / m[0]
     power, n = scale, [None, None]
@@ -803,11 +792,10 @@
     ]
     for at, value in enumerate(parts):
         coef[at : at + 1, :] = jnp.broadcast_to(value, (1, LANES))
-    coef[6:8, :] = jnp.zeros((2, LANES), jnp.float32)
     sound = (fall * LIMIT >= n[2]) & (bend * LIMIT >= n[3])
     sound = sound & (lead * LIMIT >= lead_size) & (turn * LIMIT >= turn_size)
     sound = sound & (alpha * lead * (2.0 * LIMIT) >= 1.0 + a * a * n[2] + alpha * alpha * n[4])
-    good[...] = jnp.where(sound, 1, 0)
+    coef[6:8, :] = jnp.broadcast_to(jnp.where(sound, 1.0, 0.0), (2, LANES))
     coef_scope.__exit__(None, None, None)
 
 
@@ -853,7 +841,6 @@
     height, width = kappa_field.shape
     tiles, _, slots = obs_cell.shape[1:]
     down, across = height // TILE, width // TILE
-    edges, inners = edge_and_inner(down, across)
     in_vmem = pl.BlockSpec(memory_space=pltpu.VMEM)
     in_hbm = pl.BlockSpec(memory_space=pltpu.HBM)
     tall = height + 2 * MARGIN
@@ -862,21 +849,18 @@
     pitch = count + 8
     flat = (tiles * count, slots)
     pitched = (tiles * pitch, slots)
-    edge = [
-        pltpu.VMEM((count, edges, slots), jnp.int16),
-        pltpu.VMEM((count, 2 * edges, slots), jnp.bfloat16),
-        pltpu.VMEM((count, inners, slots), jnp.int16),
-        pltpu.VMEM((count, 2 * inners, slots), jnp.bfloat16),
+    blocks = [
+        pltpu.VMEM((count, tiles, slots), jnp.int16),
+        pltpu.VMEM((count, 2 * tiles, slots), jnp.bfloat16),
     ]
-    fields, coef, good = pl.pallas_call(
+    fields, coef = pl.pallas_call(
         functools.partial(field_kernel, rows, cols),
         out_shape=(
             jax.ShapeDtypeStruct((5, across + 1, tall, LANES), jnp.float32),
             jax.ShapeDtypeStruct((8, LANES), jnp.float32),
-            jax.ShapeDtypeStruct((1, 1), jnp.int32),
         ),
         in_specs=[in_hbm] * 5,
-        out_specs=(in_vmem,) * 3,
+        out_specs=(in_vmem,) * 2,
         scratch_shapes=[
             pltpu.VMEM(flat, jnp.int32),
             pltpu.VMEM(flat, jnp.bfloat16),
@@ -885,11 +869,11 @@
             pltpu.VMEM(pitched, jnp.int32),
             pltpu.VMEM(pitched, jnp.float32),
             pltpu.VMEM(pitched, jnp.float32),
-            *edge,
-            *edge,
-            pltpu.VMEM((GROUP * edges, slots), jnp.float32),
-            pltpu.VMEM((GROUP * edges, slots), jnp.float32),
-            pltpu.VMEM((GROUP * edges * 2, slots), jnp.float32),
+            *blocks,
+            *blocks,
+            pltpu.VMEM(flat, jnp.float32),
+            pltpu.VMEM(flat, jnp.float32),
+            pltpu.VMEM((2 * tiles * count, slots), jnp.float32),
             pltpu.VMEM(wide.shape, jnp.float32),
             pltpu.VMEM(wide.shape, jnp.float32),
             pltpu.VMEM((16, height), jnp.float32),
@@ -903,8 +887,8 @@
             pltpu.VMEM((1, LANES), jnp.float32),
             pltpu.VMEM((count, 1, LANES), jnp.float32),
             pltpu.SemaphoreType.DMA((4 + across,)),
-            pltpu.SemaphoreType.DMA((2, 2)),
-            pltpu.SemaphoreType.DMA((count // GROUP, 2, 2)),
+            pltpu.SemaphoreType.DMA((2,)),
+            pltpu.SemaphoreType.DMA((len(cuts_of(count)) - 1, 2)),
             pltpu.SemaphoreType.DMA((2, 8)),
             pltpu.SemaphoreType.DMA((2, 8)),
             pltpu.SemaphoreType.DMA((2,)),
@@ -943,7 +927,7 @@
             name="hand_on",
         )(*smooth(rows, cols, own[0], own[1], kappa))
 
-    return lax.cond(good[0, 0] > 0, combine, iterate, fields, coef, kappa_field)
+    return lax.cond(coef[6, 0] > 0, combine, iterate, fields, coef, kappa_field)
 
 
 def smooth(rows, cols, response, weight_field, kappa_field):

time: 38.7 us -> 35.7 us (0.922)
  Pallas kernels: 36.9 us -> 33.4 us
  local copies, waits for them, and re-layouts: 0 us -> 0.51 us
    pallas_call x1, Pallas kernels: 35.4 us -> 31.9 us  [per_device(): pl.pallas_call(functools.partial(field_kernel, rows, cols), out_shape=(ja...]
    slice x0 -> x1, local copies, waits for them, and re-layouts: none -> 0.51 us  [per_device(): return lax.cond(coef[6, 0] > 0, combine, iterate, fields, coef, kappa_field)]
where the time goes in v3:
time: 35.7 us; the launch traced here: 35.6 us
  Pallas kernels  33.4 us (94%)
  between operations  1.45 us (4%)
  local copies, waits for them, and re-layouts  0.51 us (1%)
    pallas_call x1, Pallas kernels, per_device(): pl.pallas_call(functools.partial(field_kernel, rows, cols), out_shape=(ja...  31.9 us
    pallas_call x1, Pallas kernels, combine(): pl.pallas_call(combine_kernel, out_shape=(field, field), in_specs=[in_vme...  1.49 us

profile of v3, /device:TPU:0, one launch (start us, length us, event | category | flops | bytes accessed | tf_op | source)
XLA Modules:
  0.0 35.6 jit_solution(17326562677149119881)
XLA Ops:
  0.6 31.9 %fields.1 = (f32[5,5,544,128]{3,2,1,0:T(8,128)S(1)}, f32[8,128]{1,0:T(8,128)S(1)}) custom-call(s32[512,128]{1,0:T(8,128)} %bitcast.17, bf16[512,128]{1,0:T(8,128)(2,1)} %bitcast.18, bf16[512,128]{1,0:T(8,128)(2,1)} %bitcast.19, s32[16,32]{1,0:T(8,128)} %bitcast.20, f32[512,512]{1,0:T(8,128)} %kappa_hbm.1), custom_call_target="tpu_custom_call" | custom-call | tf_op jit(solution)/shard_map/fields/pallas_call | solution.py:856
  32.5 0.5 %slice.14 = f32[1,1]{1,0:T(1,128)} slice(f32[8,128]{1,0:T(8,128)S(1)} %get-tuple-element.18), slice={[6:7], [0:1]} | slice | bytes 8 | tf_op jit(solution)/shard_map/slice | solution.py:930
  33.7 1.7 %conditional.1 = ((f32[512,512]{1,0:T(8,128)}, f32[512,512]{1,0:T(8,128)})) conditional(s32[]{:T(128)} %bitcast.5, (f32[5,5,544,128]{3,2,1,0:T(8,128)S(1)}, f32[512,512]{1,0:T(8,128)}) %tuple.12, (f32[5,5,544,128]{3,2,1,0:T(8,128)S(1)}, f32[8,128]{1,0:T(8,128)S(1)}) %fields.1), branch_computations={%region_0.0_spmd, %region_1.0_spmd} | conditional | bytes 39092316 | solution.py:930
  33.9 1.5 %combine.1 = (f32[512,512]{1,0:T(8,128)}, f32[512,512]{1,0:T(8,128)}) custom-call(f32[5,5,544,128]{3,2,1,0:T(8,128)S(1)} %get-tuple-element.12.fields, f32[8,128]{1,0:T(8,128)S(1)} %get-tuple-element.13.coef), custom_call_target="tpu_custom_call" | custom-call | tf_op jit(solution)/shard_map/cond/branch_1_fun/combine/pallas_call | solution.py:906
